TPU v7x, 32 devices: a whole 2x2x4 slice. The times are simulated.
32 devices in a mesh: ctx: 16 (over z, x, core), head: 2 (over y).
Axes of the slice: x: 2, y: 2, z: 4, core: 2. Of those that a mesh axis runs over, the one named last changes fastest.
Arguments:
- queries: bfloat16 [8192, 4096], P(('ctx', 'head')), may hold values from -48 to 48
- keys: bfloat16 [8192, 4096], P(('ctx', 'head')), may hold values from -6 to 6
- values: bfloat16 [8192, 4096], P(('ctx', 'head')), may hold values from -6 to 6
- rates: float32 [8192, 8], P('ctx', 'head'), may hold values from 0.0003314563 to 0.003314563
- fast_gate: float32 [8, 512, 512], P('head'), may hold values from -0.25 to 0.25
- fast_up: float32 [8, 512, 512], P('head'), may hold values from -0.25 to 0.25
- fast_down: float32 [8, 512, 512], P('head'), may hold values from -0.25 to 0.25
- out_gain: float32 [4096], P('head'), may hold values from 0.5 to 1.5
Outputs:
- mixed: bfloat16 [8192, 4096], P('ctx', 'head')
All inputs are finite; a program needn't handle non-finite values.
Results may differ from a plain program's by a relative error of at most 0.012.
Values may be sent and summed in bfloat16 or wider, within the bound.
No kernel may reach another device: no remote copies, remote signals or barrier semaphores. Data moves between devices by JAX's collectives and lax.ppermute only.
A program may use at most 192 MiB of HBM per device.

v0:
```python
import math

import jax
import jax.numpy as jnp
from jax import lax
from jax.sharding import PartitionSpec as P

WINDOW = 1024
AHD = 128
FD = 512


epsilon = 1e-06
rms_epsilon = 1e-05


def passed_along(value, axis, steps):
    count = lax.axis_size(axis)
    first, last = (max(0, -steps), min(count, count - steps))
    return lax.ppermute(value, axis, [(source, source + steps) for source in range(first, last)])


def silu_slope(pre):
    sigma = jax.nn.sigmoid(pre)
    return sigma * (1.0 + pre * (1.0 - sigma))


def column_norms(matrix):
    return jnp.sqrt(jnp.sum(matrix * matrix, axis=-2) + epsilon)


def shards(queries, keys, values, rates, fast_gate, fast_up, fast_down, out_gain):
    query_here, key_here, value_here = (
        lax.all_to_all(queries, "head", split_axis=1, concat_axis=0, tiled=True),
        lax.all_to_all(keys, "head", split_axis=1, concat_axis=0, tiled=True),
        lax.all_to_all(values, "head", split_axis=1, concat_axis=0, tiled=True),
    )
    token_count = query_here.shape[0]
    width_here = query_here.shape[1]
    reach = WINDOW // token_count
    first_token = lax.axis_index("ctx") * token_count
    paired = jnp.stack([key_here, value_here])
    earlier = []
    for distance in range(reach, 0, -1):
        earlier.append(passed_along(paired, "ctx", distance))
    collected = jnp.concatenate(earlier + [paired], axis=1)
    heads_here = width_here // AHD
    span_keys = (reach + 1) * token_count
    query_heads = query_here.reshape(token_count, heads_here, AHD)
    key_heads = collected[0].reshape(span_keys, heads_here, AHD)
    value_heads = collected[1].reshape(span_keys, heads_here, AHD)
    scores = jnp.einsum(
        "qhd,khd->hqk", query_heads, key_heads, preferred_element_type=jnp.float32
    ) * (1.0 / math.sqrt(AHD))
    query_pos = first_token + jnp.arange(token_count, dtype=jnp.int32)
    key_pos = first_token - reach * token_count + jnp.arange(span_keys, dtype=jnp.int32)
    allowed = (
        (key_pos[None, :] <= query_pos[:, None])
        & (key_pos[None, :] > query_pos[:, None] - WINDOW)
        & (key_pos[None, :] >= 0)
    )
    scores = jnp.where(allowed[None], scores, -1e30)
    peak = jnp.max(scores, axis=-1, keepdims=True)
    expo = jnp.exp(scores - peak)
    weights = (expo / jnp.sum(expo, axis=-1, keepdims=True)).astype(jnp.bfloat16)
    attended = jnp.einsum(
        "hqk,khd->qhd", weights, value_heads, preferred_element_type=jnp.float32
    ).reshape(token_count, width_here)
    fast_here = width_here // FD
    query_fast = query_here.reshape(token_count, fast_here, FD)
    key_fast = key_here.reshape(token_count, fast_here, FD)
    value_fast = value_here.reshape(token_count, fast_here, FD)
    gate_cast = fast_gate.astype(jnp.bfloat16)
    up_cast = fast_up.astype(jnp.bfloat16)
    down_cast = fast_down.astype(jnp.bfloat16)
    pre_gate = jnp.einsum("thi,hij->thj", key_fast, gate_cast, preferred_element_type=jnp.float32)
    pre_up = jnp.einsum("thi,hij->thj", key_fast, up_cast, preferred_element_type=jnp.float32)
    hidden = (jax.nn.silu(pre_gate) * pre_up).astype(jnp.bfloat16)
    target = (rates[:, :, None] * value_fast.astype(jnp.float32)).astype(jnp.bfloat16)
    step_down = jnp.einsum("thi,thj->hij", hidden, target, preferred_element_type=jnp.float32)
    back = jnp.einsum("thj,hij->thi", target, down_cast, preferred_element_type=jnp.float32)
    grad_gate = (back * pre_up * silu_slope(pre_gate)).astype(jnp.bfloat16)
    grad_up = (back * jax.nn.silu(pre_gate)).astype(jnp.bfloat16)
    step_gate = jnp.einsum("thi,thj->hij", key_fast, grad_gate, preferred_element_type=jnp.float32)
    step_up = jnp.einsum("thi,thj->hij", key_fast, grad_up, preferred_element_type=jnp.float32)
    initials = (fast_gate, fast_up, fast_down)
    initial_norms = [column_norms(matrix) for matrix in initials]
    summed = lax.psum((step_gate, step_up, step_down), "ctx")
    renormed = []
    for initial, norm_before, step_value in zip(initials, initial_norms, summed):
        moved = initial + step_value
        renormed.append(
            (moved * (norm_before / column_norms(moved))[:, None, :]).astype(jnp.bfloat16)
        )
    read_gate = jnp.einsum(
        "thi,hij->thj", query_fast, renormed[0], preferred_element_type=jnp.float32
    )
    read_up = jnp.einsum(
        "thi,hij->thj", query_fast, renormed[1], preferred_element_type=jnp.float32
    )
    read_hidden = (jax.nn.silu(read_gate) * read_up).astype(jnp.bfloat16)
    read = jnp.einsum("thi,hij->thj", read_hidden, renormed[2], preferred_element_type=jnp.float32)
    scale_back = lax.rsqrt(jnp.mean(read * read, axis=-1, keepdims=True) + rms_epsilon)
    readout = read * scale_back * out_gain.reshape(fast_here, FD)[None, :, :]
    return (attended + readout.reshape(token_count, width_here)).astype(jnp.bfloat16)


def solution(mesh):
    return jax.shard_map(
        shards,
        mesh=mesh,
        in_specs=(
            P(("ctx", "head"), None),
            P(("ctx", "head"), None),
            P(("ctx", "head"), None),
            P("ctx", "head"),
            P("head", None, None),
            P("head", None, None),
            P("head", None, None),
            P("head"),
        ),
        out_specs=P("ctx", "head"),
        check_vma=False,
    )
```

profile of v0, /device:TPU:0, one launch (start us, length us, event | category | flops | bytes accessed | tf_op | source)
XLA Modules:
  0.0 492.7 jit_solution(2968835977343370354)
XLA Ops:
  6.5 3.2 copy.89
  9.7 4.3 all-to-all-start
  14.0 3.2 copy.88
  17.2 22.7 %all-to-all-done = bf16[256,2,2048]{2,0,1:T(8,128)(2,1)S(1)} async-done(((bf16[256,2,2048]{2,0,1:T(8,128)(2,1)}), bf16[256,2,2048]{2,0,1:T(8,128)(2,1)S(1)}, u32[]{:S(2)}, u32[]{:S(2)}) %all-to-all-start) | async-done | bytes 2097184 | tf_op jit(solution)/shard_map/all_to_all | solution.py:35
  39.8 1.3 copy-done.3
  41.1 3.8 all-to-all-start.1
  45.7 3.2 copy.87
  48.9 5.2 %copy.38 = f32[4,512,512]{1,2,0:T(8,128)} copy(f32[4,512,512]{2,1,0:T(8,128)} %param.12) | data formatting | bytes 8388608 | tf_op args[4]
  54.1 5.2 %copy.41 = f32[4,512,512]{1,2,0:T(8,128)} copy(f32[4,512,512]{2,1,0:T(8,128)} %param.13) | data formatting | bytes 8388608 | tf_op args[5]
  59.4 3.3 multiply_reduce_fusion.3
  62.7 6.8 %all-to-all-done.1 = bf16[256,2,2048]{2,0,1:T(8,128)(2,1)S(1)} async-done(((bf16[256,2,2048]{2,0,1:T(8,128)(2,1)}), bf16[256,2,2048]{2,0,1:T(8,128)(2,1)S(1)}, u32[]{:S(2)}, u32[]{:S(2)}) %all-to-all-start.1) | async-done | bytes 2097184 | tf_op jit(solution)/shard_map/all_to_all | solution.py:36
  69.4 4.8 all-to-all-start.2
  74.3 3.3 multiply_reduce_fusion.1
  77.6 1.1 and_and_fusion
  78.8 3.9 copy.54
  82.7 2.5 copy.55
  85.2 4.6 pad_maximum_fusion
  89.7 3.2 collective-permute-start.1
  93.0 4.0 collective-permute-start
  97.0 1.1 all-to-all-done.2
  98.0 3.3 reshape.161
  101.4 3.0 copy.51
  104.4 3.5 copy.59
  107.9 3.3 reshape.160
  111.2 6.0 %fusion.35 = f32[4,512,512]{2,1,0:T(8,128)} fusion(f32[4,512,512]{2,1,0:T(8,128)} %param.12, bf16[512,4,512]{2,1,0:T(4,128)(2,1)S(1)} %reshape.160), kind=kOutput, calls=%fused_computation.66 | convolution fusion | flops 1074790400 | bytes 10485760 | tf_op jit(solution)/shard_map/thi,hij->thj/dot_general | solution.py:76
  117.2 2.5 bitcast_convert_fusion
  119.7 6.0 %reshape.163 = f32[512,4,512]{2,1,0:T(4,128)} reshape(f32[2,256,2048]{2,1,0:T(8,128)} %bitcast_convert_fusion) | data formatting | bytes 8388608 | tf_op jit(solution)/shard_map/convert_element_type | solution.py:79
  125.7 2.9 multiply_convert_fusion.3
  129.2 1.9 fusion.33
  131.4 1.4 fusion.30
  132.7 0.8 copy-done.7
  133.6 3.6 fusion.25
  137.2 3.5 convolution_bitcast_fusion
  140.7 3.6 convolution_bitcast_fusion.1
  144.3 64.4 %collective-permute-done = bf16[2,512,2048]{1,2,0:T(8,128)(2,1)} collective-permute-done((bf16[2,512,2048]{1,2,0:T(8,128)(2,1)}, bf16[2,512,2048]{1,2,0:T(8,128)(2,1)}, u32[]{:S(2)}, u32[]{:S(2)}) %collective-permute-start) | collective-permute-done | bytes 4194336 | tf_op jit(solution)/shard_map/ppermute | solution.py:20
  208.7 5.6 %maximum_maximum_fusion = bf16[2,1536,2048]{1,2,0:T(8,128)(2,1)S(1)} fusion(bf16[1,512,2048]{1,2,0:T(8,128)(2,1)} %copy.55, bf16[1,512,2048]{1,2,0:T(8,128)(2,1)S(1)} %copy-done.4, bf16[2,512,2048]{1,2,0:T(8,128)(2,1)} %collective-permute-done.1, bf16[2,512,2048]{1,2,0:T(8,128)(2,1)} %collective-permute-done), kind=kLoop, calls=%fused_computation.9 | loop fusion | flops 50331648 | bytes 25165824 | tf_op jit(solution)/shard_map/concatenate | solution.py:46
  214.3 4.9 fusion.57
  219.2 25.7 %fusion.58 = (f32[16,512]{1,0:T(8,128)S(1)}, f32[16,512,1536]{1,2,0:T(8,128)}) fusion(pred[512,1536]{0,1:T(8,128)(4,1)S(1)} %and_and_fusion, bf16[1536,16,128]{0,2,1:T(8,128)(2,1)} %bitcast.134, bf16[512,16,128]{2,1,0:T(8,128)(2,1)S(1)} %bitcast.139), kind=kOutput, calls=%fused_computation.92 | convolution fusion | flops 3271558656 | bytes 59539456 | tf_op jit(solution)/shard_map/sub | solution.py:64
  244.9 21.6 %fusion.5 = f32[16,128,512]{2,1,0:T(8,128)} fusion(bf16[1536,16,128]{0,2,1:T(8,128)(2,1)} %bitcast.133, f32[16,512,1536]{1,2,0:T(8,128)} %get-tuple-element.18, f32[16,512]{1,0:T(8,128)S(1)} %get-tuple-element.17), kind=kOutput, calls=%fused_computation.8 | convolution fusion | flops 3246391296 | bytes 60850176 | tf_op jit(solution)/shard_map/hqk,khd->qhd/dot_general | solution.py:66
  266.5 5.4 %copy.44 = f32[512,2048]{1,0:T(8,128)} copy(f32[512,2048]{0,1:T(8,128)} %bitcast.135) | data formatting | bytes 8388608 | tf_op jit(solution)/shard_map/reshape | solution.py:68
  271.9 167.3 %all-reduce.3.cloned.1.call-done = (f32[4,512,512]{2,1,0:T(8,128)}, f32[4,512,512]{1,2,0:T(8,128)}, f32[4,512,512]{1,2,0:T(8,128)}) async-done(((f32[4,512,512]{2,1,0:T(8,128)}, f32[4,512,512]{1,2,0:T(8,128)}, f32[4,512,512]{1,2,0:T(8,128)}), (f32[4,512,512]{2,1,0:T(8,128)}, f32[4,512,512]{1,2,0:T(8,128)}, f32[4,512,512]{1,2,0:T(8,128)})) %all-reduce.3.cloned.1.call-update) | async-done | bytes 12582928 | tf_op jit(solution)/shard_map/psum | solution.py:88
  439.2 6.5 %multiply_reduce_fusion.4 = (f32[4,512]{1,0:T(4,128)S(1)}, f32[4,512,512]{2,1,0:T(8,128)}, f32[4,512]{1,0:T(4,128)S(1)}) fusion(f32[4,512,512]{2,1,0:T(8,128)} %param.14, f32[4,512,512]{2,1,0:T(8,128)} %get-tuple-element.5), kind=kLoop, calls=%fused_computation.46 | loop fusion | flops 5238784 | bytes 12599296 | tf_op jit(solution)/shard_map/reduce_sum | solution.py:29
  445.7 9.7 %multiply_reduce_fusion = (f32[4,512]{1,0:T(4,128)S(1)}, f32[4,512,512]{1,2,0:T(8,128)}, f32[4,512]{1,0:T(4,128)S(1)}, f32[4,512,512]{1,2,0:T(8,128)}) fusion(f32[4,512,512]{1,2,0:T(8,128)} %copy.41, f32[4,512,512]{1,2,0:T(8,128)} %get-tuple-element.7, f32[4,512,512]{1,2,0:T(8,128)} %copy.38, f32[4,512,512]{1,2,0:T(8,128)} %get-tuple-element.6), kind=kLoop, calls=%fused_computation.40 | loop fusion | flops 6287360 | bytes 25182208 | tf_op jit(solution)/shard_map/reduce_sum | solution.py:29
  455.5 5.4 %fusion.24 = f32[4,512,512]{2,1,0:T(8,128)} fusion(bf16[512,4,512]{0,2,1:T(8,128)(2,1)S(1)} %copy-done.6, f32[4,512,512]{1,2,0:T(8,128)} %get-tuple-element.24, f32[4,512]{1,0:T(4,128)S(1)} %rsqrt_multiply_fusion.1), kind=kOutput, calls=%fused_computation.53 | convolution fusion | flops 1075838976 | bytes 10493952 | tf_op jit(solution)/shard_map/thi,hij->thj/dot_general | solution.py:95
  460.9 9.5 %fusion.8 = (f32[512,4]{0,1:T(4,128)S(1)}, f32[4,512,512]{2,1,0:T(8,128)}) fusion(f32[4,512,512]{2,1,0:T(8,128)} %fusion.24, bf16[512,4,512]{0,2,1:T(8,128)(2,1)S(1)} %copy-done.6, f32[4,512,512]{1,2,0:T(8,128)} %get-tuple-element.9, f32[4,512]{1,0:T(4,128)S(1)} %rsqrt_multiply_fusion, f32[4,512,512]{2,1,0:T(8,128)} %get-tuple-element.13, ...), kind=kOutput, calls=%fused_computation.14 | convolution fusion | flops 2160064512 | bytes 18898944 | tf_op jit(solution)/shard_map/thi,hij->thj/dot_general | solution.py:102
  470.4 4.6 fusion.9
  475.0 5.4 %copy.45 = f32[512,2048]{1,0:T(8,128)} copy(f32[512,2048]{0,1:T(8,128)} %bitcast.129) | data formatting | bytes 8388608 | tf_op jit(solution)/shard_map/reshape | solution.py:105
  480.4 5.4 %add_convert_fusion = bf16[512,2048]{1,0:T(8,128)(2,1)} fusion(f32[512,2048]{1,0:T(8,128)} %copy.44, f32[512,2048]{1,0:T(8,128)} %copy.45), kind=kLoop, calls=%fused_computation.38 | loop fusion | flops 2097152 | bytes 10485760 | tf_op jit(solution)/shard_map/convert_element_type | solution.py:105
  (38 shorter events, 1.8 us)
Async XLA Ops:
  9.7 30.1 %all-to-all-start = ((bf16[256,2,2048]{2,0,1:T(8,128)(2,1)}), bf16[256,2,2048]{2,0,1:T(8,128)(2,1)S(1)}, u32[]{:S(2)}, u32[]{:S(2)}) async-start(bf16[256,2,2048]{2,0,1:T(8,128)(2,1)} %bitcast.132), calls=%async_computation | async-start | bytes 4194304 | tf_op jit(solution)/shard_map/all_to_all | solution.py:35
  14.0 31.0 %copy-start.13 = (f32[2048]{0:T(1024)S(1)}, f32[2048]{0:T(1024)}, u32[]{:S(2)}) copy-start(f32[2048]{0:T(1024)} %param.15) | copy-start | bytes 24580
  14.0 31.6 %copy-start.12 = (f32[512,4]{0,1:T(4,128)S(1)}, f32[512,4]{0,1:T(4,128)}, u32[]{:S(2)}) copy-start(f32[512,4]{0,1:T(4,128)} %param.11) | copy-start | bytes 24580
  39.8 1.3 copy-start.3
  41.1 28.3 %all-to-all-start.1 = ((bf16[256,2,2048]{2,0,1:T(8,128)(2,1)}), bf16[256,2,2048]{2,0,1:T(8,128)(2,1)S(1)}, u32[]{:S(2)}, u32[]{:S(2)}) async-start(bf16[256,2,2048]{2,0,1:T(8,128)(2,1)} %bitcast.131), calls=%async_computation.1 | async-start | bytes 4194304 | tf_op jit(solution)/shard_map/all_to_all | solution.py:36
  69.4 13.2 %copy-start.1 = (bf16[256,2,2048]{2,0,1:T(8,128)(2,1)}, bf16[256,2,2048]{2,0,1:T(8,128)(2,1)S(1)}, u32[]{:S(2)}) copy-start(bf16[256,2,2048]{2,0,1:T(8,128)(2,1)S(1)} %all-to-all-done.1) | copy-start | bytes 6291460
  69.4 28.6 %all-to-all-start.2 = ((bf16[256,2,2048]{2,0,1:T(8,128)(2,1)}), bf16[256,2,2048]{2,0,1:T(8,128)(2,1)}, u32[]{:S(2)}, u32[]{:S(2)}) async-start(bf16[256,2,2048]{2,0,1:T(8,128)(2,1)} %bitcast.130), calls=%async_computation.2 | async-start | bytes 4194304 | tf_op jit(solution)/shard_map/all_to_all | solution.py:34
  74.3 364.9 %all-reduce.3.cloned.1.call-start = ((), (), s32[]{:S(2)}) async-start(), calls=%async_computation.3 | async-start | bytes 25165824 | tf_op jit(solution)/shard_map/psum | solution.py:88
  89.7 54.6 %collective-permute-start.1 = (bf16[2,512,2048]{1,2,0:T(8,128)(2,1)}, bf16[2,512,2048]{1,2,0:T(8,128)(2,1)}, u32[]{:S(2)}, u32[]{:S(2)}) collective-permute-start(bf16[2,512,2048]{1,2,0:T(8,128)(2,1)} %pad_maximum_fusion), channel_id=1, source_target_pairs={{0,2},{2,4},{4,6},{6,8},{8,10},{10,12},{12,14},{14,16},{16,18},{18... | collective-permute-start | bytes 12582920 | tf_op jit(solution)/shard_map/ppermute | solution.py:20
  93.0 115.8 %collective-permute-start = (bf16[2,512,2048]{1,2,0:T(8,128)(2,1)}, bf16[2,512,2048]{1,2,0:T(8,128)(2,1)}, u32[]{:S(2)}, u32[]{:S(2)}) collective-permute-start(bf16[2,512,2048]{1,2,0:T(8,128)(2,1)} %pad_maximum_fusion), channel_id=1, source_target_pairs={{0,4},{2,6},{4,8},{6,10},{8,12},{10,14},{12,16},{14,18},{16,20},{1... | collective-permute-start | bytes 12582920 | tf_op jit(solution)/shard_map/ppermute | solution.py:20
  111.2 6.0 %copy-start.2 = (bf16[256,2,2048]{2,0,1:T(8,128)(2,1)S(1)}, bf16[256,2,2048]{2,0,1:T(8,128)(2,1)}, u32[]{:S(2)}) copy-start(bf16[256,2,2048]{2,0,1:T(8,128)(2,1)} %copy-done.1) | copy-start | bytes 6291460
  125.7 3.4 copy-start
  129.2 2.2 copy-start.5
  131.4 2.2 copy-start.7
  144.3 64.4 %copy-start.4 = (bf16[1,512,2048]{1,2,0:T(8,128)(2,1)S(1)}, bf16[1,512,2048]{1,2,0:T(8,128)(2,1)}, u32[]{:S(2)}) copy-start(bf16[1,512,2048]{1,2,0:T(8,128)(2,1)} %copy.54) | copy-start | bytes 6291460
  214.3 4.9 copy-start.8
  445.7 9.7 %copy-start.9 = (f32[4,512]{1,0:T(4,128)S(1)}, f32[4,512]{1,0:T(4,128)}, u32[]{:S(2)}) copy-start(f32[4,512]{1,0:T(4,128)} %multiply_reduce_fusion.3) | copy-start | bytes 24580
  445.7 9.7 %copy-start.10 = (f32[4,512]{1,0:T(4,128)S(1)}, f32[4,512]{1,0:T(4,128)}, u32[]{:S(2)}) copy-start(f32[4,512]{1,0:T(4,128)} %multiply_reduce_fusion.1) | copy-start | bytes 24580
  445.7 9.7 %copy-start.6 = (bf16[512,4,512]{0,2,1:T(8,128)(2,1)S(1)}, bf16[512,4,512]{0,2,1:T(8,128)(2,1)}, u32[]{:S(2)}) copy-start(bf16[512,4,512]{0,2,1:T(8,128)(2,1)} %copy.51) | copy-start | bytes 6291460
  460.9 9.5 %copy-start.11 = (f32[4,512]{1,0:T(4,128)S(1)}, f32[4,512]{1,0:T(4,128)}, u32[]{:S(2)}) copy-start(f32[4,512]{1,0:T(4,128)} %mul.142) | copy-start | bytes 24580
Sparse Core Ops, SparseCore 0:
  144.5 294.6 all-reduce.2
where the time goes:
time: 494 us; the launch traced here: 493 us
  waiting for transfers between devices  262 us (53%)
  matrix products  82.2 us (17%)
  local copies, waits for them, and re-layouts  65.1 us (13%)
  other arithmetic  49.4 us (10%)
  starting transfers between devices  20.1 us (4%)
  between operations  13.6 us (3%)
    psum x1, waiting for transfers between devices, shards(): summed = lax.psum((step_gate, step_up, step_down), 'ctx')  167 us
    ppermute x2, waiting for transfers between devices, passed_along(): lax.ppermute(value, axis, [(source, source + steps) for source in range(f...  64.4 us
    sub x1, matrix products, shards(): expo = jnp.exp(scores - peak)  25.7 us
    reduce_sum x4, other arithmetic, column_norms(): return jnp.sqrt(jnp.sum(matrix * matrix, axis=-2) + epsilon)  22.8 us
    all_to_all x1, waiting for transfers between devices, shards(): lax.all_to_all(keys, 'head', split_axis=1, concat_axis=0, tiled=True)  22.7 us
    dot_general x1, matrix products, shards(): jnp.einsum('hqk,khd->qhd', weights, value_heads, preferred_element_type=j...  21.6 us
    unnamed x32, local copies, waits for them, and re-layouts  17.2 us
  transfers between devices with their start and end apart: 6, of which 5 were waited for; matrix products, arithmetic and copies ran while one was open for 29% of the time, Pallas kernels for 0%

commit v1 on v0

v1 whole, which is shorter than its diff:
```python
import functools
import math

import jax
import jax.numpy as jnp
from jax import lax
from jax.experimental import pallas as pl
from jax.experimental.pallas import tpu as pltpu
from jax.sharding import Mesh, PartitionSpec as P


WINDOW = 1024
AHD = 128
FD = 512
BLOCK = 256
ROWS = 512

epsilon = 1e-06
rms_epsilon = 1e-05

f32 = jnp.float32
bf16 = jnp.bfloat16


def dot(a, b, dims):
    return lax.dot_general(a, b, (dims, ((), ())), preferred_element_type=f32)


NN = ((1,), (0,))
NT = ((1,), (1,))
TN = ((0,), (0,))

LOCAL = pl.BlockSpec(memory_space=pltpu.VMEM)


def attention_body(which, *rest, run, early, block, count):
    query_pieces, pieces = rest[:count], rest[count : 2 * count]
    early_refs = rest[2 * count : 2 * count + early]
    out_ref, query_all, key_all, value_all = rest[-4:]
    rows = query_pieces[0].shape[1]
    for over in range(count):
        source = lax.bitwise_xor(which[2], over) * rows
        query_all[pl.ds(pl.multiple_of(source, rows), rows), :] = query_pieces[over][0]
        here = pl.ds(pl.multiple_of(source + WINDOW, rows), rows)
        key_all[here, :] = pieces[over][0]
        value_all[here, :] = pieces[over][1]
    for over, early_ref in enumerate(early_refs):
        source = lax.rem(lax.bitwise_xor(which[2], over), early) * rows
        here = pl.ds(pl.multiple_of(source, rows), rows)
        key_all[here, :] = early_ref[0]
        value_all[here, :] = early_ref[1]
    q_ref = query_all.at[run * WINDOW : (run + 1) * WINDOW]
    kp_ref, vp_ref = (ref.at[run * WINDOW : (run + 1) * WINDOW] for ref in (key_all, value_all))
    kc_ref, vc_ref = (ref.at[(run + 1) * WINDOW : (run + 2) * WINDOW] for ref in (key_all, value_all))
    rows = q_ref.shape[0]
    before = kp_ref.shape[0]
    present = which[1] if early else 1
    factor = math.log2(math.e) / math.sqrt(AHD)
    bias = jnp.where(present > 0, 0.0, -1e30).astype(f32)
    own = lax.broadcasted_iota(jnp.int32, (block, block), 1) <= lax.broadcasted_iota(
        jnp.int32, (block, block), 0
    )
    for at in range(0, rows, block):
        end = at + block
        query = q_ref[at:end, :]
        score_p = dot(query, kp_ref[at:before, :], NT)
        score_c = dot(query, kc_ref[0:end, :], NT)
        pieces = [(jnp.where(own, score_c[:, at:end], score_p[:, :block] + bias), None)]
        if at + block < before:
            pieces.append((score_p[:, block:], bias))
        if at:
            pieces.append((score_c[:, :at], None))
        peak = None
        for score, shift in pieces:
            top = jnp.max(score, axis=-1, keepdims=True)
            if shift is not None:
                top = top + shift
            peak = top if peak is None else jnp.maximum(peak, top)
        peak = peak * factor
        expos = []
        total = None
        for score, shift in pieces:
            level = peak if shift is None else peak - shift
            expo = jnp.exp2(score * factor - level)
            part = jnp.sum(expo, axis=-1, keepdims=True)
            total = part if total is None else total + part
            expos.append(expo.astype(bf16))
        mixed = expos.pop(0)
        zero = jnp.zeros_like(mixed)
        result = dot(jnp.where(own, mixed, zero), vc_ref[at:end, :], NN)
        result += dot(jnp.where(own, zero, mixed), vp_ref[at:end, :], NN)
        if end < before:
            result += dot(expos.pop(0), vp_ref[end:before, :], NN)
        if at:
            result += dot(expos.pop(0), vc_ref[0:at, :], NN)
        out_ref[at:end, :] = result / total


def attention_call(which, queries, pieces, early, out, run):
    count = len(queries)
    _, rows, width = queries[0].shape
    tokens = count * rows
    heads = width // AHD
    block = min(BLOCK, WINDOW)
    pairs = heads * WINDOW * (WINDOW + block)
    given = [*queries, *pieces, *early]
    in_specs = [pl.BlockSpec((*piece.shape[:2], AHD), lambda h, _: (0, 0, h)) for piece in given]
    args = [which, *(in_hbm(piece) for piece in given)]
    aliases = {}
    if out is not None:
        in_specs.append(pl.BlockSpec(memory_space=pl.ANY))
        aliases = {len(args): 0}
        args.append(out)
    return pl.pallas_call(
        functools.partial(
            attention_body, run=run, early=len(early), block=block, count=count
        ),
        out_shape=jax.ShapeDtypeStruct((tokens, width), f32),
        grid_spec=pltpu.PrefetchScalarGridSpec(
            num_scalar_prefetch=1,
            grid=(heads,),
            in_specs=in_specs,
            out_specs=pl.BlockSpec((WINDOW, AHD), lambda h, _: (run, h)),
            scratch_shapes=[
                pltpu.VMEM((tokens, AHD), bf16),
                pltpu.VMEM((tokens + WINDOW, AHD), bf16),
                pltpu.VMEM((tokens + WINDOW, AHD), bf16),
            ],
        ),
        input_output_aliases=aliases,
        compiler_params=pltpu.CompilerParams(
            dimension_semantics=("arbitrary",), vmem_limit_bytes=40 << 20
        ),
        cost_estimate=pl.CostEstimate(
            flops=pairs * AHD * 4, transcendentals=pairs, bytes_accessed=tokens * width * 14
        ),
        name="attention",
    )(*args)


def update_body(which, rate_ref, *rest, overs, before, parts):
    count = len(overs)
    pieces, matrices = rest[:count], rest[count : count + 3]
    outs, steps = rest[count + 3 + before :], rest[-1]
    if before:
        outs = outs[:-1]
    rows = pieces[0].shape[1]
    gate, up, down = (matrix[...] for matrix in matrices)
    together = max(1, min(ROWS // rows, count))

    def joined(arrays):
        return arrays[0] if len(arrays) == 1 else jnp.concatenate(arrays, axis=0)

    for first in range(0, count, together):
        taken = range(first, min(first + together, count))
        places = [pl.multiple_of(lax.bitwise_xor(which[2], overs[at]) * rows, rows) for at in taken]
        rate = joined([rate_ref[pl.ds(at, rows), :] for at in places])
        key = joined([pieces[at][0] for at in taken])
        value = joined([pieces[at][1] for at in taken])
        pre_gate = dot(key, gate, NN)
        pre_up = dot(key, up, NN)
        target = (rate * value.astype(f32)).astype(bf16)
        back = dot(target, down, NT)
        sigma = jax.nn.sigmoid(pre_gate)
        silu = pre_gate * sigma
        hidden = (silu * pre_up).astype(bf16)
        grad_up = (back * silu).astype(bf16)
        grad_gate = (back * pre_up * (sigma * (1.0 + pre_gate * (1.0 - sigma)))).astype(bf16)
        for at, step in enumerate((dot(key, grad_gate, TN), dot(key, grad_up, TN), dot(hidden, target, TN))):
            if first:
                steps[at] += step
            elif before:
                steps[at] = rest[count + 3][at] + step
            else:
                steps[at] = step
    if parts == 1:
        outs[0][...] = steps[...]
    elif parts:
        wide = FD // parts
        for ahead, out_ref in enumerate(outs):
            at = lax.rem(which[1] + ahead, parts) * wide
            out_ref[...] = steps[:, :, pl.ds(pl.multiple_of(at, wide), wide)].astype(out_ref.dtype)


def update_call(which, overs, pieces, rate, matrices, earlier, parts):
    tokens = len(pieces) * pieces[0].shape[1]
    shape = (3, FD, FD // max(parts, 1))
    if parts:
        out_shape = [jax.ShapeDtypeStruct(shape, bf16 if ahead else f32) for ahead in range(parts)]
        scratch = [pltpu.VMEM((3, FD, FD), f32)]
    else:
        out_shape = [jax.ShapeDtypeStruct(shape, f32)]
        scratch = []
    args = [rate, *pieces, *matrices, *earlier]
    return pl.pallas_call(
        functools.partial(update_body, overs=overs, before=len(earlier), parts=parts),
        out_shape=out_shape,
        grid_spec=pltpu.PrefetchScalarGridSpec(
            num_scalar_prefetch=1,
            grid=(1,),
            in_specs=[LOCAL] * len(args),
            out_specs=[LOCAL] * len(out_shape),
            scratch_shapes=scratch,
        ),
        compiler_params=pltpu.CompilerParams(
            dimension_semantics=("arbitrary",), vmem_limit_bytes=52 << 20
        ),
        cost_estimate=pl.CostEstimate(
            flops=tokens * FD * FD * 12, transcendentals=tokens * FD, bytes_accessed=tokens * FD * 4 + FD * FD * 18
        ),
        name="update",
    )(which, *args)


def in_hbm(value):
    return pltpu.with_memory_space_constraint(value, pltpu.HBM)


def renorm_body(which, gate_ref, up_ref, down_ref, *rest):
    *got, out_ref = rest
    for at, initial_ref in enumerate((gate_ref, up_ref, down_ref)):
        initial = initial_ref[0]
        moved = initial
        for got_ref in got:
            moved = moved + got_ref[at].astype(f32)
        norm_before = jnp.sqrt(jnp.sum(initial * initial, axis=0, keepdims=True) + epsilon)
        norm_after = jnp.sqrt(jnp.sum(moved * moved, axis=0, keepdims=True) + epsilon)
        out_ref[at] = (moved * (norm_before / norm_after)).astype(bf16)


def renorm_call(which, got, gate, up, down):
    shape = got[0].shape
    wide = shape[-1]
    matrix = pl.BlockSpec((1, FD, wide), lambda i, w: (w[0], 0, w[1]))
    piece = pl.BlockSpec(shape, lambda i, w: (0, 0, 0))
    return pl.pallas_call(
        renorm_body,
        out_shape=jax.ShapeDtypeStruct(shape, bf16),
        grid_spec=pltpu.PrefetchScalarGridSpec(
            num_scalar_prefetch=1,
            grid=(1,),
            in_specs=[matrix] * 3 + [piece] * len(got),
            out_specs=piece,
        ),
        compiler_params=pltpu.CompilerParams(vmem_limit_bytes=32 << 20),
        cost_estimate=pl.CostEstimate(flops=FD * wide * 3 * 12, transcendentals=0, bytes_accessed=FD * wide * 3 * 20),
        name="renorm",
    )(which, in_hbm(gate), in_hbm(up), in_hbm(down), *got)


def readout_body(which, block, gain_ref, attended_ref, *rest, count):
    queries = rest[:count]
    *pieces, out_ref, weights = rest[count:]
    rows = queries[0].shape[1]
    wide = FD // len(pieces)
    for back, piece_ref in enumerate(pieces):
        column = lax.rem(which[1] + len(pieces) - back, len(pieces)) * wide
        weights[:, :, pl.ds(pl.multiple_of(column, wide), wide)] = piece_ref[...]
    query = queries[0][0] if count == 1 else jnp.concatenate([ref[0] for ref in queries], axis=0)
    gate = dot(query, weights[0], NN)
    up = dot(query, weights[1], NN)
    hidden = (gate * jax.nn.sigmoid(gate) * up).astype(bf16)
    read = dot(hidden, weights[2], NN)
    scale_back = lax.rsqrt(jnp.mean(read * read, axis=-1, keepdims=True) + rms_epsilon)
    readout = read * scale_back * gain_ref[...]
    for at in range(count):
        source = lax.rem(lax.bitwise_xor(which[2], at), count) * rows
        here = pl.ds(pl.multiple_of(source, rows), rows)
        out_ref[here, :] = (attended_ref[here, :] + readout[at * rows : (at + 1) * rows]).astype(bf16)


def readout_call(which, block, queries, pieces, attended, gain):
    count = len(queries)
    rows = count * queries[0].shape[1]

    def whole(array):
        return pl.BlockSpec(array.shape, lambda i, w, b: (0,) * array.ndim)

    return pl.pallas_call(
        functools.partial(readout_body, count=count),
        out_shape=jax.ShapeDtypeStruct((rows, FD), bf16),
        grid_spec=pltpu.PrefetchScalarGridSpec(
            num_scalar_prefetch=2,
            grid=(1,),
            in_specs=[whole(gain), pl.BlockSpec((rows, FD), lambda i, w, b: (b[0], 0))]
            + [whole(array) for array in (*queries, *pieces)],
            out_specs=pl.BlockSpec((rows, FD), lambda i, w, b: (0, 0)),
            scratch_shapes=[pltpu.VMEM((3, FD, FD), bf16)],
        ),
        compiler_params=pltpu.CompilerParams(
            dimension_semantics=("arbitrary",), vmem_limit_bytes=40 << 20
        ),
        cost_estimate=pl.CostEstimate(
            flops=rows * FD * FD * 6, transcendentals=rows * FD, bytes_accessed=rows * FD * 8 + FD * FD * 6
        ),
        name="readout",
    )(which, block, gain, in_hbm(attended), *queries, *pieces)


def spread_body(which, *rest, kinds, halves, subs):
    arrays, outs, sems = rest[:kinds], rest[kinds:-1], rest[-1]
    copies = []
    for over, out_ref in enumerate(outs):
        target = lax.bitwise_xor(which[2], over)
        at = pl.multiple_of((lax.rem(target, halves) * subs + lax.div(target, halves)) * FD, FD)
        for kind, array in enumerate(arrays):
            copies.append(
                pltpu.make_async_copy(array.at[:, pl.ds(at, FD)], out_ref.at[kind], sems.at[kind, over])
            )
            copies[-1].start()
    for copy in copies:
        copy.wait()


def spread_call(which, arrays, halves, subs):
    count, kinds = halves * subs, len(arrays)
    shape = (kinds, arrays[0].shape[0], FD)
    return pl.pallas_call(
        functools.partial(spread_body, kinds=kinds, halves=halves, subs=subs),
        out_shape=[jax.ShapeDtypeStruct(shape, bf16)] * count,
        grid_spec=pltpu.PrefetchScalarGridSpec(
            num_scalar_prefetch=1,
            grid=(1,),
            in_specs=[pl.BlockSpec(memory_space=pltpu.HBM)] * kinds,
            out_specs=[LOCAL] * count,
            scratch_shapes=[pltpu.SemaphoreType.DMA((kinds, count))],
        ),
        cost_estimate=pl.CostEstimate(
            flops=count * math.prod(shape), transcendentals=0, bytes_accessed=count * math.prod(shape) * 4
        ),
        name="spread",
    )(which, *arrays)


def arrange_body(which, *rest):
    *pieces, out_ref = rest
    rows = pieces[0].shape[1]
    for over, piece in enumerate(pieces):
        source = lax.bitwise_xor(which[2], over) * rows
        out_ref[:, pl.ds(pl.multiple_of(source, rows), rows), :] = piece[...]


def arrange_call(which, pieces):
    count = len(pieces)
    kinds, rows, _ = pieces[0].shape
    return pl.pallas_call(
        arrange_body,
        out_shape=jax.ShapeDtypeStruct((kinds, count * rows, FD), bf16),
        grid_spec=pltpu.PrefetchScalarGridSpec(
            num_scalar_prefetch=1,
            grid=(1,),
            in_specs=[LOCAL] * count,
            out_specs=LOCAL,
        ),
        name="arrange",
    )(which, *pieces)


def planned(queries, keys, values, rates, fast_gate, fast_up, fast_down, out_gain):
    groups, subs, halves = (lax.axis_size(axis) for axis in ("grp", "sub", "head"))
    group, sub, half = (lax.axis_index(axis) for axis in ("grp", "sub", "head"))
    rows = queries.shape[0]
    members = subs * halves
    tokens = rows * members

    place = sub * halves + half
    top = members // 2
    which = jnp.stack([sub, group, place]).astype(jnp.int32)
    order = []
    for over in range(top):
        order += [over + top] + [over + 1] * (over + 1 < top)

    def sent(piece, over):
        links = [(source, source ^ over) for source in range(members)]
        return lax.ppermute(piece, ("sub", "head"), links)

    def spread(arrays):
        return list(spread_call(which, arrays, halves, subs))

    def from_earlier(value):
        size = value.shape[0]
        reach = -(-WINDOW // size)
        pieces = []
        for distance in range(min(reach, groups - 1), 0, -1):
            count = min(size, WINDOW - (distance - 1) * size)
            links = [(source, source + distance) for source in range(groups - distance)]
            pieces.append(lax.ppermute(value[size - count :], "grp", links))
        short = WINDOW - sum(piece.shape[0] for piece in pieces)
        if short:
            pieces.insert(0, jnp.zeros((short, FD), value.dtype))
        return pieces[0] if len(pieces) == 1 else jnp.concatenate(pieces)

    def to_sub(value, over):
        return lax.ppermute(value, "sub", [(source, source ^ over) for source in range(subs)])

    def to_group(value, ahead):
        return lax.ppermute(value, "grp", [(source, (source + ahead) % groups) for source in range(groups)])

    by_sub = rates.T
    slots = []
    for over in range(subs):
        wanted = lax.dynamic_index_in_dim(by_sub, sub ^ over, 0, keepdims=False)
        slots.append(to_sub(wanted, over) if over else wanted)
    slots = jnp.stack(slots)
    rate = jnp.concatenate([lax.dynamic_index_in_dim(slots, sub ^ at, 0, keepdims=False) for at in range(subs)])
    rate = rate.reshape(tokens, 1)

    pieces = spread([keys, values])
    for over in order:
        pieces[over] = sent(pieces[over], over)
    query_pieces = spread([queries])
    for over in order:
        query_pieces[over] = sent(query_pieces[over], over)

    halved = top * rows == WINDOW
    if halved:
        links = [(source, source + 1) for source in range(groups - 1)]
        early = []
        for over in range(top):
            late = jnp.where(place >= top, pieces[over], pieces[over + top])
            early.append(lax.ppermute(late, "grp", links))

    parts = groups if FD % (groups * 128) == 0 else 1
    matrices = [
        lax.dynamic_index_in_dim(matrix, sub, 0, keepdims=False).astype(bf16)
        for matrix in (fast_gate, fast_up, fast_down)
    ]
    last = [over for over in range(members) if over % top == top - 1]
    most = [over for over in range(members) if over % top != top - 1]

    def updated(overs, earlier, parts):
        return update_call(which, overs, [pieces[over] for over in overs], rate, matrices, earlier, parts)

    begun = updated(most, [], 0)
    steps = updated(last, begun, parts)

    if parts > 1:
        got = [steps[0]] + [to_group(steps[ahead], ahead) for ahead in range(1, parts)]
        mine = renorm_call(which, got, fast_gate, fast_up, fast_down)
        weights = [mine] + [to_group(mine, ahead) for ahead in range(1, parts)]
    else:
        whole = jnp.stack([sub, sub * 0]).astype(jnp.int32)
        got = [lax.psum(steps[0], "grp") if groups > 1 else steps[0]]
        weights = [renorm_call(whole, got, fast_gate, fast_up, fast_down)]

    if halved:
        attended = attention_call(which, query_pieces, pieces, [], None, 1)
        attended = attention_call(which, query_pieces, pieces, early, attended, 0)
    else:
        key, value = arrange_call(which, pieces)
        (query,) = arrange_call(which, query_pieces)
        early_key = from_earlier(key)
        early_value = from_earlier(value)
        attended = short_attention(group, query, early_key, key, early_value, value)

    slots = [None] * subs
    gain = lax.dynamic_slice_in_dim(out_gain, sub * FD, FD).reshape(1, FD)
    for over in range(subs - 1, -1, -1):
        block = (sub ^ over).astype(jnp.int32)[None]
        chosen = query_pieces[over * halves : (over + 1) * halves]
        mixed = readout_call(which, block, chosen, weights, attended, gain)
        slots[over] = to_sub(mixed, over) if over else mixed
    if subs == 1:
        return slots[0]
    out = None
    for overs in ((0, 1), *((over,) for over in range(subs - 1, 1, -1))):
        out = join_call(which, overs, [slots[over] for over in overs], out, subs)
    return out


def join_body(which, *rest, overs):
    slots, (out_ref, sems) = rest[: len(overs)], rest[-2:]
    copies = []
    for number, over in enumerate(overs):
        at = pl.multiple_of(lax.bitwise_xor(which[0], over) * FD, FD)
        copies.append(pltpu.make_async_copy(slots[number], out_ref.at[:, pl.ds(at, FD)], sems.at[number]))
        copies[-1].start()
    for copy in copies:
        copy.wait()


def join_call(which, overs, slots, out, subs):
    raw = pl.BlockSpec(memory_space=pltpu.HBM)
    given = list(slots) if out is None else [*slots, out]
    return pl.pallas_call(
        functools.partial(join_body, overs=overs),
        out_shape=jax.ShapeDtypeStruct((slots[0].shape[0], FD * subs), bf16),
        grid_spec=pltpu.PrefetchScalarGridSpec(
            num_scalar_prefetch=1,
            grid=(1,),
            in_specs=[LOCAL] * len(slots) + [raw] * (len(given) - len(slots)),
            out_specs=raw,
            scratch_shapes=[pltpu.SemaphoreType.DMA((len(slots),))],
        ),
        input_output_aliases={} if out is None else {1 + len(slots): 0},
        name="join",
    )(which, *given)


def short_body(group_ref, q_ref, kp_ref, kc_ref, vp_ref, vc_ref, out_ref):
    rows, before = q_ref.shape[0], kp_ref.shape[0]
    factor = 1.0 / math.sqrt(AHD)
    query = q_ref[...]
    at = lax.broadcasted_iota(jnp.int32, (rows, before), 0)
    back = lax.broadcasted_iota(jnp.int32, (rows, before), 1)
    score_p = dot(query, kp_ref[...], NT) * factor
    score_p = jnp.where((back > at) & (back >= before - group_ref[0] * rows), score_p, -1e30)
    own = lax.broadcasted_iota(jnp.int32, (rows, rows), 1) <= lax.broadcasted_iota(jnp.int32, (rows, rows), 0)
    score_c = jnp.where(own, dot(query, kc_ref[...], NT) * factor, -1e30)
    peak = jnp.maximum(jnp.max(score_p, axis=-1, keepdims=True), jnp.max(score_c, axis=-1, keepdims=True))
    expo_p, expo_c = jnp.exp(score_p - peak), jnp.exp(score_c - peak)
    total = jnp.sum(expo_p, axis=-1, keepdims=True) + jnp.sum(expo_c, axis=-1, keepdims=True)
    result = dot(expo_p.astype(bf16), vp_ref[...], NN) + dot(expo_c.astype(bf16), vc_ref[...], NN)
    out_ref[...] = result / total


def short_attention(group, q, kp, kc, vp, vc):
    tokens, width = q.shape
    here = pl.BlockSpec((tokens, AHD), lambda h, _: (0, h))
    prior = pl.BlockSpec((WINDOW, AHD), lambda h, _: (0, h))
    return pl.pallas_call(
        short_body,
        out_shape=jax.ShapeDtypeStruct((tokens, width), f32),
        grid_spec=pltpu.PrefetchScalarGridSpec(
            num_scalar_prefetch=1,
            grid=(width // AHD,),
            in_specs=[here, prior, here, prior, here],
            out_specs=here,
        ),
        compiler_params=pltpu.CompilerParams(dimension_semantics=("arbitrary",), vmem_limit_bytes=40 << 20),
        name="short_attention",
    )(group.astype(jnp.int32)[None], q, kp, kc, vp, vc)


def solution(mesh):
    contexts, halves = mesh.shape["ctx"], mesh.shape["head"]

    def run(queries, keys, values, rates, fast_gate, fast_up, fast_down, out_gain):
        subs = fast_gate.shape[0] // halves
        split = Mesh(mesh.devices.reshape(contexts // subs, subs, halves), ("grp", "sub", "head"))
        rows = P(("grp", "sub", "head"), None)
        matrix = P("head", None, None)
        step = jax.shard_map(
            planned,
            mesh=split,
            in_specs=(rows, rows, rows, P(("grp", "sub"), "head"), matrix, matrix, matrix, P("head")),
            out_specs=P(("grp", "sub"), "head"),
            check_vma=False,
        )
        return step(queries, keys, values, rates, fast_gate, fast_up, fast_down, out_gain)

    return run
```

time: 494 us -> 218 us (0.44)
  the two profiles are of different devices: /device:TPU:0 before, /device:TPU:24 now
where the time goes in v1:
time: 218 us; the launch traced here: 217 us
  waiting for transfers between devices  83.4 us (38%)
  Pallas kernels  74.4 us (34%)
  starting transfers between devices  36.2 us (17%)
  local copies, waits for them, and re-layouts  16.4 us (8%)
  other arithmetic  6.19 us (3%)
    ppermute x6, waiting for transfers between devices, to_group(): lax.ppermute(value, 'grp', [(source, (source + ahead) % groups) for sourc...  46.8 us
    pallas_call x2, Pallas kernels, attention_call(): pl.pallas_call(functools.partial(attention_body, run=run, early=len(early...  25.8 us
    ppermute x14, waiting for transfers between devices, sent(): return lax.ppermute(piece, ('sub', 'head'), links)  24.7 us
    pallas_call x2, Pallas kernels, update_call(): pl.pallas_call(functools.partial(update_body, overs=overs, before=len(ear...  17.6 us
    ppermute x14, starting transfers between devices, sent(): return lax.ppermute(piece, ('sub', 'head'), links)  15.3 us
    pallas_call x4, Pallas kernels, readout_call(): pl.pallas_call(functools.partial(readout_body, count=count), out_shape=ja...  12.5 us
    ppermute x6, starting transfers between devices, to_group(): lax.ppermute(value, 'grp', [(source, (source + ahead) % groups) for sourc...  11.5 us
    unnamed x78, local copies, waits for them, and re-layouts  9.51 us
  transfers between devices with their start and end apart: 30, of which 10 were waited for; matrix products, arithmetic and copies ran while one was open for 6% of the time, Pallas kernels for 29%

profile of v1, /device:TPU:24, one launch (start us, length us, event | category | flops | bytes accessed | tf_op | source)
XLA Modules:
  0.0 217.3 jit_solution(17230608404010380956)
XLA Ops:
  0.6 5.0 %spread.3 = (bf16[2,256,512]{2,1,0:T(8,128)(2,1)}, bf16[2,256,512]{2,1,0:T(8,128)(2,1)}, bf16[2,256,512]{2,1,0:T(8,128)(2,1)}, bf16[2,256,512]{2,1,0:T(8,128)(2,...) custom-call(s32[3]{0:T(128)} %pad_add_fusion.which, ...), custom_call_target="tpu_custom_call" | custom-call | flops 2097152 | bytes 8388608 | tf_op jit(solution)/shard_map/spread/pallas_call | solution.py:318
  5.7 1.6 collective-permute-start.7
  7.3 1.5 collective-permute-start.10
  10.7 2.7 %fusion = (bf16[512,512]{1,0:T(8,128)(2,1)}, bf16[512,512]{1,0:T(8,128)(2,1)}) fusion(f32[4,512,512]{2,1,0:T(8,128)} %gate_ref.1, s32[]{:T(128)S(6)} %select_n.50, f32[4,512,512]{2,1,0:T(8,128)} %up_ref.1), kind=kLoop, calls=%fused_computation.3 | loop fusion | bytes 2097156 | tf_op jit(solution)/shard_map/convert_element_type | solution.py:425
  13.4 2.1 fusion.2.rest_8_.rest_4_
  15.5 3.6 %spread.2 = (bf16[1,256,512]{2,1,0:T(8,128)(2,1)}, bf16[1,256,512]{2,1,0:T(8,128)(2,1)}, bf16[1,256,512]{2,1,0:T(8,128)(2,1)}, bf16[1,256,512]{2,1,0:T(8,128)(2,...) custom-call(s32[3]{0:T(128)} %pad_add_fusion.which, ...), custom_call_target="tpu_custom_call" | custom-call | flops 1048576 | bytes 4194304 | tf_op jit(solution)/shard_map/spread/pallas_call | solution.py:318
  20.0 1.0 collective-permute-start.8
  21.0 1.4 collective-permute-start.11
  22.5 1.3 copy.13.rate_ref
  23.9 1.8 collective-permute-start.9
  25.7 1.0 collective-permute-start.13
  27.5 1.3 collective-permute-start
  28.9 7.9 %collective-permute-done.11.rest_13_.rest_4_ = bf16[2,256,512]{2,1,0:T(8,128)(2,1)S(1)} collective-permute-done((bf16[2,256,512]{2,1,0:T(8,128)(2,1)S(1)}, bf16[2,256,512]{2,1,0:T(8,128)(2,1)S(1)}, u32[]{:S(2)}, u32[]{:S(2)}) %collective-permute-start.11) | collective-permute-done | bytes 524320 | tf_op jit(solution)/shard_map/ppermute | solution.py:375
  36.8 9.4 %collective-permute-done.12.rest_14_.rest_5_ = bf16[2,256,512]{2,1,0:T(8,128)(2,1)} collective-permute-done((bf16[2,256,512]{2,1,0:T(8,128)(2,1)}, bf16[2,256,512]{2,1,0:T(8,128)(2,1)}, u32[]{:S(2)}, u32[]{:S(2)}) %collective-permute-start.12) | collective-permute-done | bytes 524320 | tf_op jit(solution)/shard_map/ppermute | solution.py:375
  46.2 2.1 collective-permute-start.2
  48.3 10.4 %update.2.rest_5_ = f32[3,512,512]{2,1,0:T(8,128)} custom-call(s32[3]{0:T(128)S(1)} %copy-done.26, f32[2048,1]{1,0:T(8,128)} %copy.13.rate_ref, bf16[2,256,512]{2,1,0:T(8,128)(2,1)S(1)} %copy-done.2, bf16[2,256,512]{2,1,0:T(8,128)(2,1)S(1)} %collective-permute-done.7.rest_9_.rest_1_, bf16[2,256,512]{2,1,0:T(8,128)(2,1)S(1)} %collective-permute-done.8.rest_10_.rest_2_, ...), custom_call_target="tpu_custom_call" | custom-call | flops 4831838208 | bytes 7864320 | tf_op jit(solution)/shard_map/update/pallas_call | solution.py:195
  58.8 1.6 collective-permute-start.3
  61.2 7.1 %update.3 = (f32[3,512,128]{2,1,0:T(8,128)}, bf16[3,512,128]{2,1,0:T(8,128)(2,1)S(1)}, bf16[3,512,128]{2,1,0:T(8,128)(2,1)S(1)}, bf16[3,512,128]{2,1,0:T(8,128)(2,1)S(1)}) custom-call(s32[3]{0:T(128)S(1)} %copy-done.26, f32[2048,1]{1,0:T(8,128)} %copy.13.rate_ref, bf16[2,256,512]{2,1,0:T(8,128)(2,1)S(1)} %collective-permute-done.9.rest_11_.rest_0_, ...), custom_call_target="tpu_custom_call" | custom-call | flops 1610612736 | bytes 5767168 | tf_op jit(solution)/shard_map/update/pallas_call | solution.py:195
  69.7 5.4 %collective-permute-done.2.rest_3_.rest_1_ = bf16[1,256,512]{2,1,0:T(8,128)(2,1)S(1)} collective-permute-done((bf16[1,256,512]{2,1,0:T(8,128)(2,1)}, bf16[1,256,512]{2,1,0:T(8,128)(2,1)S(1)}, u32[]{:S(2)}, u32[]{:S(2)}) %collective-permute-start.2) | collective-permute-done | bytes 262176 | tf_op jit(solution)/shard_map/ppermute | solution.py:375
  75.9 1.9 broadcast_select_fusion.1
  77.8 1.3 collective-permute-start.14
  79.1 1.3 collective-permute-start.15
  80.4 1.9 broadcast_select_fusion
  82.3 1.3 collective-permute-start.16
  83.6 22.8 %collective-permute-done.22.rest_2_ = bf16[3,512,128]{2,1,0:T(8,128)(2,1)S(1)} collective-permute-done((bf16[3,512,128]{2,1,0:T(8,128)(2,1)S(1)}, bf16[3,512,128]{2,1,0:T(8,128)(2,1)S(1)}, u32[]{:S(2)}, u32[]{:S(2)}) %collective-permute-start.22) | collective-permute-done | bytes 393248 | tf_op jit(solution)/shard_map/ppermute | solution.py:397
  107.2 1.3 collective-permute-start.17
  109.3 1.2 collective-permute-start.6
  111.2 1.1 copy-done.21
  112.4 1.0 copy-done.23
  113.4 1.0 copy-done.25
  114.4 2.1 renorm.1.rest_2_
  116.5 2.0 collective-permute-done.6.rest_7_.rest_1_
  118.6 2.4 %collective-permute-start.24 = (bf16[3,512,128]{2,1,0:T(8,128)(2,1)S(1)}, bf16[3,512,128]{2,1,0:T(8,128)(2,1)S(1)}, u32[]{:S(2)}, u32[]{:S(2)}) collective-permute-start(bf16[3,512,128]{2,1,0:T(8,128)(2,1)S(1)} %renorm.1.rest_2_), channel_id=1, source_target_pairs={{0,8},{8,16},{16,24},{24,0},{1,9},{9,17},{17,25},{25,1},{2,10},{10... | collective-permute-start | bytes 1179656 | tf_op jit(solution)/shard_map/ppermute | solution.py:397
  121.0 2.0 collective-permute-start.25
  123.5 6.1 %collective-permute-start.26 = (bf16[3,512,128]{2,1,0:T(8,128)(2,1)S(1)}, bf16[3,512,128]{2,1,0:T(8,128)(2,1)S(1)}, u32[]{:S(2)}, u32[]{:S(2)}) collective-permute-start(bf16[3,512,128]{2,1,0:T(8,128)(2,1)S(1)} %renorm.1.rest_2_), channel_id=1, source_target_pairs={{0,24},{8,0},{16,8},{24,16},{1,25},{9,1},{17,9},{25,17},{2,26},{10... | collective-permute-start | bytes 1179656 | tf_op jit(solution)/shard_map/ppermute | solution.py:397
  129.6 12.7 %attention.2.rest_20_ = f32[2048,512]{1,0:T(8,128)S(1)} custom-call(s32[3]{0:T(128)S(1)} %copy-done.26, bf16[1,256,512]{2,1,0:T(8,128)(2,1)} %get-tuple-element.25.rest_0_, bf16[1,256,512]{2,1,0:T(8,128)(2,1)} %copy-done.6, bf16[1,256,512]{2,1,0:T(8,128)(2,1)} %copy-done.8, bf16[1,256,512]{2,1,0:T(8,128)(2,1)} %copy-done.10, ...), custom_call_target="tpu_custom_call" | custom-call | flops 2684354560 | bytes 14680064 | tf_op jit(solution)/shard_map/attention/pallas_call | solution.py:114
  142.3 3.6 %collective-permute-done.17.rest_19_ = bf16[2,256,512]{2,1,0:T(8,128)(2,1)} collective-permute-done((bf16[2,256,512]{2,1,0:T(8,128)(2,1)}, bf16[2,256,512]{2,1,0:T(8,128)(2,1)}, u32[]{:S(2)}, u32[]{:S(2)}) %collective-permute-start.17) | collective-permute-done | bytes 524320 | tf_op jit(solution)/shard_map/ppermute | solution.py:421
  145.9 13.1 %attention.3.attended_ref = f32[2048,512]{1,0:T(8,128)S(1)} custom-call(s32[3]{0:T(128)S(1)} %copy-done.26, bf16[1,256,512]{2,1,0:T(8,128)(2,1)} %get-tuple-element.25.rest_0_, bf16[1,256,512]{2,1,0:T(8,128)(2,1)} %copy-done.6, bf16[1,256,512]{2,1,0:T(8,128)(2,1)} %copy-done.8, bf16[1,256,512]{2,1,0:T(8,128)(2,1)} %copy-done.10, ...), custom_call_target="tpu_custom_call", output_to_operand_aliasing={{}: (21, {})} | custom-call | flops 2684354560 | bytes 14680064 | tf_op jit(solution)/shard_map/attention/pallas_call | solution.py:114
  159.1 2.0 copy-done
  161.1 24.0 %collective-permute-done.25.rest_4_ = bf16[3,512,128]{2,1,0:T(8,128)(2,1)S(1)} collective-permute-done((bf16[3,512,128]{2,1,0:T(8,128)(2,1)S(1)}, bf16[3,512,128]{2,1,0:T(8,128)(2,1)S(1)}, u32[]{:S(2)}, u32[]{:S(2)}) %collective-permute-start.25) | collective-permute-done | bytes 393248 | tf_op jit(solution)/shard_map/ppermute | solution.py:397
  185.1 3.1 %readout.5 = bf16[512,512]{1,0:T(8,128)(2,1)S(1)} custom-call(s32[3]{0:T(128)S(1)} %copy-done.26, s32[1]{0:T(128)} %bitcast.20.block, f32[1,512]{1,0:T(1,128)S(1)} %bitcast.26, f32[2048,512]{1,0:T(8,128)} %copy-done, bf16[1,256,512]{2,1,0:T(8,128)(2,1)S(1)} %copy-done.17, bf16[1,256,512]{2,1,0:T(8,128)(2,1)S(1)} %copy-done.19, ...), custom_call_target="tpu_custom_call" | custom-call | flops 805306368 | bytes 3670016 | tf_op jit(solution)/shard_map/readout/pallas_call | solution.py:279
  189.2 3.1 %readout.7 = bf16[512,512]{1,0:T(8,128)(2,1)S(1)} custom-call(s32[3]{0:T(128)S(1)} %copy-done.26, s32[1]{0:T(128)} %bitcast.21.block, f32[1,512]{1,0:T(1,128)S(1)} %bitcast.27, f32[2048,512]{1,0:T(8,128)} %copy-done, bf16[1,256,512]{2,1,0:T(8,128)(2,1)S(1)} %copy-done.9, bf16[1,256,512]{2,1,0:T(8,128)(2,1)S(1)} %copy-done.11, ...), custom_call_target="tpu_custom_call" | custom-call | flops 805306368 | bytes 3670016 | tf_op jit(solution)/shard_map/readout/pallas_call | solution.py:279
  192.9 3.1 %readout.4 = bf16[512,512]{1,0:T(8,128)(2,1)S(1)} custom-call(s32[3]{0:T(128)S(1)} %copy-done.26, s32[1]{0:T(128)} %bitcast.3.block, f32[1,512]{1,0:T(1,128)S(1)} %bitcast.28, f32[2048,512]{1,0:T(8,128)} %copy-done, bf16[1,256,512]{2,1,0:T(8,128)(2,1)S(1)} %copy-done.13, bf16[1,256,512]{2,1,0:T(8,128)(2,1)S(1)} %copy-done.15, ...), custom_call_target="tpu_custom_call" | custom-call | flops 805306368 | bytes 3670016 | tf_op jit(solution)/shard_map/readout/pallas_call | solution.py:279
  196.9 3.1 %readout.6.rest_0_ = bf16[512,512]{1,0:T(8,128)(2,1)S(1)} custom-call(s32[3]{0:T(128)S(1)} %copy-done.26, s32[1]{0:T(128)} %bitcast.block, f32[1,512]{1,0:T(1,128)S(1)} %bitcast.29, f32[2048,512]{1,0:T(8,128)} %copy-done, bf16[1,256,512]{2,1,0:T(8,128)(2,1)S(1)} %copy-done.5, bf16[1,256,512]{2,1,0:T(8,128)(2,1)S(1)} %copy-done.7, ...), custom_call_target="tpu_custom_call" | custom-call | flops 805306368 | bytes 3670016 | tf_op jit(solution)/shard_map/readout/pallas_call | solution.py:279
  200.8 2.8 %join.3.rest_1_ = bf16[512,2048]{1,0:T(8,128)(2,1)} custom-call(s32[3]{0:T(128)} %pad_add_fusion.which, bf16[512,512]{1,0:T(8,128)(2,1)} %copy-done.20, bf16[512,512]{1,0:T(8,128)(2,1)} %collective-permute-done.29.rest_1_), custom_call_target="tpu_custom_call" | custom-call | tf_op jit(solution)/shard_map/join/pallas_call | solution.py:485
  204.5 2.5 %join.4.rest_1_ = bf16[512,2048]{1,0:T(8,128)(2,1)} custom-call(s32[3]{0:T(128)} %pad_add_fusion.which, bf16[512,512]{1,0:T(8,128)(2,1)} %copy-done.32, bf16[512,2048]{1,0:T(8,128)(2,1)} %join.3.rest_1_), custom_call_target="tpu_custom_call", output_to_operand_aliasing={{}: (2, {})} | custom-call | tf_op jit(solution)/shard_map/join/pallas_call | solution.py:485
  207.0 6.7 %collective-permute-done.27.rest_0_ = bf16[512,512]{1,0:T(8,128)(2,1)S(1)} collective-permute-done((bf16[512,512]{1,0:T(8,128)(2,1)S(1)}, bf16[512,512]{1,0:T(8,128)(2,1)S(1)}, u32[]{:S(2)}, u32[]{:S(2)}) %collective-permute-start.27) | collective-permute-done | bytes 524320 | tf_op jit(solution)/shard_map/ppermute | solution.py:394
  214.6 2.5 %join.5 = bf16[512,2048]{1,0:T(8,128)(2,1)} custom-call(s32[3]{0:T(128)} %pad_add_fusion.which, bf16[512,512]{1,0:T(8,128)(2,1)} %copy-done.33, bf16[512,2048]{1,0:T(8,128)(2,1)} %join.4.rest_1_), custom_call_target="tpu_custom_call", output_to_operand_aliasing={{}: (2, {})} | custom-call | tf_op jit(solution)/shard_map/join/pallas_call | solution.py:485
  (117 shorter events, 15.1 us)
Async XLA Ops:
  5.7 15.4 %copy-start.35 = (bf16[2,256,512]{2,1,0:T(8,128)(2,1)S(1)}, bf16[2,256,512]{2,1,0:T(8,128)(2,1)}, u32[]{:S(2)}) copy-start(bf16[2,256,512]{2,1,0:T(8,128)(2,1)} %get-tuple-element.38) | copy-start | bytes 1572868
  5.7 21.0 %copy-start.2 = (bf16[2,256,512]{2,1,0:T(8,128)(2,1)S(1)}, bf16[2,256,512]{2,1,0:T(8,128)(2,1)}, u32[]{:S(2)}) copy-start(bf16[2,256,512]{2,1,0:T(8,128)(2,1)} %get-tuple-element.33.rest_8_.rest_0_) | copy-start | bytes 1572868
  5.7 42.6 %copy-start.26 = (s32[3]{0:T(128)S(1)}, s32[3]{0:T(128)}, u32[]{:S(2)}) copy-start(s32[3]{0:T(128)} %pad_add_fusion.which) | copy-start | bytes 40
  5.7 18.2 %collective-permute-start.7 = (bf16[2,256,512]{2,1,0:T(8,128)(2,1)}, bf16[2,256,512]{2,1,0:T(8,128)(2,1)S(1)}, u32[]{:S(2)}, u32[]{:S(2)}) collective-permute-start(bf16[2,256,512]{2,1,0:T(8,128)(2,1)} %get-tuple-element.34), channel_id=1, source_target_pairs={{0,1},{1,0},{2,3},{3,2},{4,5},{5,4},{6,7},{7,6},{8,9},{9,8},{10,11... | collective-permute-start | bytes 1572872 | tf_op jit(solution)/shard_map/ppermute | solution.py:375
  7.3 18.4 %collective-permute-start.10 = (bf16[2,256,512]{2,1,0:T(8,128)(2,1)}, bf16[2,256,512]{2,1,0:T(8,128)(2,1)S(1)}, u32[]{:S(2)}, u32[]{:S(2)}) collective-permute-start(bf16[2,256,512]{2,1,0:T(8,128)(2,1)} %get-tuple-element.37), channel_id=1, source_target_pairs={{0,4},{1,5},{2,6},{3,7},{4,0},{5,1},{6,2},{7,3},{8,12},{9,13},{10,... | collective-permute-start | bytes 1572872 | tf_op jit(solution)/shard_map/ppermute | solution.py:375
  8.8 11.2 %collective-permute-start.20 = (f32[512]{0:T(512)S(1)}, f32[512]{0:T(512)S(1)}, u32[]{:S(2)}, u32[]{:S(2)}) collective-permute-start(f32[512]{0:T(512)S(1)} %bitcast.37), channel_id=1, source_target_pairs={{0,6},{2,4},{4,2},{6,0},{1,7},{3,5},{5,3},{7,1},{8,14},{10,12},{12... | collective-permute-start | bytes 6152 | tf_op jit(solution)/shard_map/ppermute | solution.py:394
  8.9 12.2 %collective-permute-start.19 = (f32[512]{0:T(512)S(1)}, f32[512]{0:T(512)S(1)}, u32[]{:S(2)}, u32[]{:S(2)}) collective-permute-start(f32[512]{0:T(512)S(1)} %bitcast.36), channel_id=1, source_target_pairs={{0,4},{2,6},{4,0},{6,2},{1,5},{3,7},{5,1},{7,3},{8,12},{10,14},{12... | collective-permute-start | bytes 6152 | tf_op jit(solution)/shard_map/ppermute | solution.py:394
  9.8 12.7 %collective-permute-start.18 = (f32[512]{0:T(512)S(1)}, f32[512]{0:T(512)S(1)}, u32[]{:S(2)}, u32[]{:S(2)}) collective-permute-start(f32[512]{0:T(512)S(1)} %bitcast.35), channel_id=1, source_target_pairs={{0,2},{2,0},{4,6},{6,4},{1,3},{3,1},{5,7},{7,5},{8,10},{10,8},{12,... | collective-permute-start | bytes 6152 | tf_op jit(solution)/shard_map/ppermute | solution.py:394
  20.0 7.5 %collective-permute-start.8 = (bf16[2,256,512]{2,1,0:T(8,128)(2,1)}, bf16[2,256,512]{2,1,0:T(8,128)(2,1)S(1)}, u32[]{:S(2)}, u32[]{:S(2)}) collective-permute-start(bf16[2,256,512]{2,1,0:T(8,128)(2,1)} %get-tuple-element.35), channel_id=1, source_target_pairs={{0,2},{1,3},{2,0},{3,1},{4,6},{5,7},{6,4},{7,5},{8,10},{9,11},{10,... | collective-permute-start | bytes 1572872 | tf_op jit(solution)/shard_map/ppermute | solution.py:375
  21.0 15.7 %collective-permute-start.11 = (bf16[2,256,512]{2,1,0:T(8,128)(2,1)S(1)}, bf16[2,256,512]{2,1,0:T(8,128)(2,1)S(1)}, u32[]{:S(2)}, u32[]{:S(2)}) collective-permute-start(bf16[2,256,512]{2,1,0:T(8,128)(2,1)S(1)} %copy-done.35), channel_id=1, source_target_pairs={{0,5},{1,4},{2,7},{3,6},{4,1},{5,0},{6,3},{7,2},{8,13},{9,12},{10,... | collective-permute-start | bytes 1572872 | tf_op jit(solution)/shard_map/ppermute | solution.py:375
  22.5 23.7 %collective-permute-start.12 = (bf16[2,256,512]{2,1,0:T(8,128)(2,1)}, bf16[2,256,512]{2,1,0:T(8,128)(2,1)}, u32[]{:S(2)}, u32[]{:S(2)}) collective-permute-start(bf16[2,256,512]{2,1,0:T(8,128)(2,1)} %get-tuple-element.39), channel_id=1, source_target_pairs={{0,6},{1,7},{2,4},{3,5},{4,2},{5,3},{6,0},{7,1},{8,14},{9,15},{10,... | collective-permute-start | bytes 1572872 | tf_op jit(solution)/shard_map/ppermute | solution.py:375
  23.9 44.5 %copy-start.3 = (bf16[2,256,512]{2,1,0:T(8,128)(2,1)}, bf16[2,256,512]{2,1,0:T(8,128)(2,1)S(1)}, u32[]{:S(2)}) copy-start(bf16[2,256,512]{2,1,0:T(8,128)(2,1)S(1)} %collective-permute-done.7.rest_9_.rest_1_) | copy-start | bytes 1572868
  23.9 34.9 %collective-permute-start.9 = (bf16[2,256,512]{2,1,0:T(8,128)(2,1)}, bf16[2,256,512]{2,1,0:T(8,128)(2,1)S(1)}, u32[]{:S(2)}, u32[]{:S(2)}) collective-permute-start(bf16[2,256,512]{2,1,0:T(8,128)(2,1)} %get-tuple-element.36), channel_id=1, source_target_pairs={{0,3},{1,2},{2,1},{3,0},{4,7},{5,6},{6,5},{7,4},{8,11},{9,10},{10,... | collective-permute-start | bytes 1572872 | tf_op jit(solution)/shard_map/ppermute | solution.py:375
  25.7 22.6 %copy-start.28 = (bf16[2,256,512]{2,1,0:T(8,128)(2,1)}, bf16[2,256,512]{2,1,0:T(8,128)(2,1)S(1)}, u32[]{:S(2)}) copy-start(bf16[2,256,512]{2,1,0:T(8,128)(2,1)S(1)} %collective-permute-done.10.rest_12_.rest_3_) | copy-start | bytes 1572868
  25.7 34.7 %collective-permute-start.13 = (bf16[2,256,512]{2,1,0:T(8,128)(2,1)}, bf16[2,256,512]{2,1,0:T(8,128)(2,1)S(1)}, u32[]{:S(2)}, u32[]{:S(2)}) collective-permute-start(bf16[2,256,512]{2,1,0:T(8,128)(2,1)} %get-tuple-element.40), channel_id=1, source_target_pairs={{0,7},{1,6},{2,5},{3,4},{4,3},{5,2},{6,1},{7,0},{8,15},{9,14},{10,... | collective-permute-start | bytes 1572872 | tf_op jit(solution)/shard_map/ppermute | solution.py:375
  27.5 48.4 %copy-start.4 = (bf16[2,256,512]{2,1,0:T(8,128)(2,1)}, bf16[2,256,512]{2,1,0:T(8,128)(2,1)S(1)}, u32[]{:S(2)}) copy-start(bf16[2,256,512]{2,1,0:T(8,128)(2,1)S(1)} %collective-permute-done.8.rest_10_.rest_2_) | copy-start | bytes 1572868
  27.5 41.7 %collective-permute-start = (bf16[1,256,512]{2,1,0:T(8,128)(2,1)}, bf16[1,256,512]{2,1,0:T(8,128)(2,1)S(1)}, u32[]{:S(2)}, u32[]{:S(2)}) collective-permute-start(bf16[1,256,512]{2,1,0:T(8,128)(2,1)} %get-tuple-element.26), channel_id=1, source_target_pairs={{0,1},{1,0},{2,3},{3,2},{4,5},{5,4},{6,7},{7,6},{8,9},{9,8},{10,11... | collective-permute-start | bytes 786440 | tf_op jit(solution)/shard_map/ppermute | solution.py:375
  36.8 32.7 %collective-permute-start.1 = (bf16[1,256,512]{2,1,0:T(8,128)(2,1)}, bf16[1,256,512]{2,1,0:T(8,128)(2,1)S(1)}, u32[]{:S(2)}, u32[]{:S(2)}) collective-permute-start(bf16[1,256,512]{2,1,0:T(8,128)(2,1)} %get-tuple-element.27), channel_id=1, source_target_pairs={{0,2},{1,3},{2,0},{3,1},{4,6},{5,7},{6,4},{7,5},{8,10},{9,11},{10,... | collective-permute-start | bytes 786440 | tf_op jit(solution)/shard_map/ppermute | solution.py:375
  46.2 28.9 %collective-permute-start.2 = (bf16[1,256,512]{2,1,0:T(8,128)(2,1)}, bf16[1,256,512]{2,1,0:T(8,128)(2,1)S(1)}, u32[]{:S(2)}, u32[]{:S(2)}) collective-permute-start(bf16[1,256,512]{2,1,0:T(8,128)(2,1)} %get-tuple-element.28), channel_id=1, source_target_pairs={{0,3},{1,2},{2,1},{3,0},{4,7},{5,6},{6,5},{7,4},{8,11},{9,10},{10,... | collective-permute-start | bytes 786440 | tf_op jit(solution)/shard_map/ppermute | solution.py:375
  58.8 21.7 %copy-start.1 = (bf16[2,256,512]{2,1,0:T(8,128)(2,1)}, bf16[2,256,512]{2,1,0:T(8,128)(2,1)S(1)}, u32[]{:S(2)}) copy-start(bf16[2,256,512]{2,1,0:T(8,128)(2,1)S(1)} %collective-permute-done.9.rest_11_.rest_0_) | copy-start | bytes 1572868
  58.8 16.6 %collective-permute-start.3 = (bf16[1,256,512]{2,1,0:T(8,128)(2,1)S(1)}, bf16[1,256,512]{2,1,0:T(8,128)(2,1)S(1)}, u32[]{:S(2)}, u32[]{:S(2)}) collective-permute-start(bf16[1,256,512]{2,1,0:T(8,128)(2,1)S(1)} %copy-done.38), channel_id=1, source_target_pairs={{0,4},{1,5},{2,6},{3,7},{4,0},{5,1},{6,2},{7,3},{8,12},{9,13},{10,... | collective-permute-start | bytes 786440 | tf_op jit(solution)/shard_map/ppermute | solution.py:375
  60.3 17.5 %collective-permute-start.4 = (bf16[1,256,512]{2,1,0:T(8,128)(2,1)S(1)}, bf16[1,256,512]{2,1,0:T(8,128)(2,1)S(1)}, u32[]{:S(2)}, u32[]{:S(2)}) collective-permute-start(bf16[1,256,512]{2,1,0:T(8,128)(2,1)S(1)} %copy-done.37), channel_id=1, source_target_pairs={{0,5},{1,4},{2,7},{3,6},{4,1},{5,0},{6,3},{7,2},{8,13},{9,12},{10,... | collective-permute-start | bytes 786440 | tf_op jit(solution)/shard_map/ppermute | solution.py:375
  69.2 47.2 %copy-start.6 = (bf16[1,256,512]{2,1,0:T(8,128)(2,1)}, bf16[1,256,512]{2,1,0:T(8,128)(2,1)S(1)}, u32[]{:S(2)}) copy-start(bf16[1,256,512]{2,1,0:T(8,128)(2,1)S(1)} %collective-permute-done.rest_1_) | copy-start | bytes 786436
  69.2 9.9 %collective-permute-start.5 = (bf16[1,256,512]{2,1,0:T(8,128)(2,1)S(1)}, bf16[1,256,512]{2,1,0:T(8,128)(2,1)S(1)}, u32[]{:S(2)}, u32[]{:S(2)}) collective-permute-start(bf16[1,256,512]{2,1,0:T(8,128)(2,1)S(1)} %copy-done.36), channel_id=1, source_target_pairs={{0,6},{1,7},{2,4},{3,5},{4,2},{5,3},{6,0},{7,1},{8,14},{9,15},{10,... | collective-permute-start | bytes 786440 | tf_op jit(solution)/shard_map/ppermute | solution.py:375
  69.4 47.0 %copy-start.8 = (bf16[1,256,512]{2,1,0:T(8,128)(2,1)}, bf16[1,256,512]{2,1,0:T(8,128)(2,1)S(1)}, u32[]{:S(2)}) copy-start(bf16[1,256,512]{2,1,0:T(8,128)(2,1)S(1)} %collective-permute-done.1.rest_2_.rest_0_) | copy-start | bytes 786436
  69.4 12.9 %collective-permute-start.21 = (bf16[3,512,128]{2,1,0:T(8,128)(2,1)S(1)}, bf16[3,512,128]{2,1,0:T(8,128)(2,1)S(1)}, u32[]{:S(2)}, u32[]{:S(2)}) collective-permute-start(bf16[3,512,128]{2,1,0:T(8,128)(2,1)S(1)} %get-tuple-element.42), channel_id=1, source_target_pairs={{0,8},{8,16},{16,24},{24,0},{1,9},{9,17},{17,25},{25,1},{2,10},{10... | collective-permute-start | bytes 1179656 | tf_op jit(solution)/shard_map/ppermute | solution.py:397
  75.1 41.4 %copy-start.10 = (bf16[1,256,512]{2,1,0:T(8,128)(2,1)}, bf16[1,256,512]{2,1,0:T(8,128)(2,1)S(1)}, u32[]{:S(2)}) copy-start(bf16[1,256,512]{2,1,0:T(8,128)(2,1)S(1)} %collective-permute-done.2.rest_3_.rest_1_) | copy-start | bytes 786436
  75.1 31.4 %collective-permute-start.22 = (bf16[3,512,128]{2,1,0:T(8,128)(2,1)S(1)}, bf16[3,512,128]{2,1,0:T(8,128)(2,1)S(1)}, u32[]{:S(2)}, u32[]{:S(2)}) collective-permute-start(bf16[3,512,128]{2,1,0:T(8,128)(2,1)S(1)} %get-tuple-element.43), channel_id=1, source_target_pairs={{0,16},{8,24},{16,0},{24,8},{1,17},{9,25},{17,1},{25,9},{2,18},{10... | collective-permute-start | bytes 1179656 | tf_op jit(solution)/shard_map/ppermute | solution.py:397
  75.4 41.1 %copy-start.12 = (bf16[1,256,512]{2,1,0:T(8,128)(2,1)}, bf16[1,256,512]{2,1,0:T(8,128)(2,1)S(1)}, u32[]{:S(2)}) copy-start(bf16[1,256,512]{2,1,0:T(8,128)(2,1)S(1)} %collective-permute-done.3.rest_4_.rest_0_) | copy-start | bytes 786436
  75.4 33.1 %collective-permute-start.23 = (bf16[3,512,128]{2,1,0:T(8,128)(2,1)S(1)}, bf16[3,512,128]{2,1,0:T(8,128)(2,1)S(1)}, u32[]{:S(2)}, u32[]{:S(2)}) collective-permute-start(bf16[3,512,128]{2,1,0:T(8,128)(2,1)S(1)} %get-tuple-element.44), channel_id=1, source_target_pairs={{0,24},{8,0},{16,8},{24,16},{1,25},{9,1},{17,9},{25,17},{2,26},{10... | collective-permute-start | bytes 1179656 | tf_op jit(solution)/shard_map/ppermute | solution.py:397
  77.8 38.7 %copy-start.14 = (bf16[1,256,512]{2,1,0:T(8,128)(2,1)}, bf16[1,256,512]{2,1,0:T(8,128)(2,1)S(1)}, u32[]{:S(2)}) copy-start(bf16[1,256,512]{2,1,0:T(8,128)(2,1)S(1)} %collective-permute-done.4.rest_5_.rest_1_) | copy-start | bytes 786436
  77.8 43.1 %collective-permute-start.14 = (bf16[2,256,512]{2,1,0:T(8,128)(2,1)}, bf16[2,256,512]{2,1,0:T(8,128)(2,1)S(1)}, u32[]{:S(2)}, u32[]{:S(2)}) collective-permute-start(bf16[2,256,512]{2,1,0:T(8,128)(2,1)} %broadcast_select_fusion.3), channel_id=1, source_target_pairs={{0,8},{8,16},{16,24},{1,9},{9,17},{17,25},{2,10},{10,18},{18,26},{... | collective-permute-start | bytes 1572872 | tf_op jit(solution)/shard_map/ppermute | solution.py:421
  79.1 37.4 %copy-start.16 = (bf16[1,256,512]{2,1,0:T(8,128)(2,1)}, bf16[1,256,512]{2,1,0:T(8,128)(2,1)S(1)}, u32[]{:S(2)}) copy-start(bf16[1,256,512]{2,1,0:T(8,128)(2,1)S(1)} %collective-permute-done.5.rest_6_.rest_0_) | copy-start | bytes 786436
  79.1 44.4 %collective-permute-start.15 = (bf16[2,256,512]{2,1,0:T(8,128)(2,1)}, bf16[2,256,512]{2,1,0:T(8,128)(2,1)}, u32[]{:S(2)}, u32[]{:S(2)}) collective-permute-start(bf16[2,256,512]{2,1,0:T(8,128)(2,1)} %broadcast_select_fusion.2), channel_id=1, source_target_pairs={{0,8},{8,16},{16,24},{1,9},{9,17},{17,25},{2,10},{10,18},{18,26},{... | collective-permute-start | bytes 1572872 | tf_op jit(solution)/shard_map/ppermute | solution.py:421
  82.3 60.0 %collective-permute-start.16 = (bf16[2,256,512]{2,1,0:T(8,128)(2,1)}, bf16[2,256,512]{2,1,0:T(8,128)(2,1)}, u32[]{:S(2)}, u32[]{:S(2)}) collective-permute-start(bf16[2,256,512]{2,1,0:T(8,128)(2,1)} %broadcast_select_fusion.1), channel_id=1, source_target_pairs={{0,8},{8,16},{16,24},{1,9},{9,17},{17,25},{2,10},{10,18},{18,26},{... | collective-permute-start | bytes 1572872 | tf_op jit(solution)/shard_map/ppermute | solution.py:421
  107.2 38.8 %collective-permute-start.17 = (bf16[2,256,512]{2,1,0:T(8,128)(2,1)}, bf16[2,256,512]{2,1,0:T(8,128)(2,1)}, u32[]{:S(2)}, u32[]{:S(2)}) collective-permute-start(bf16[2,256,512]{2,1,0:T(8,128)(2,1)} %broadcast_select_fusion), channel_id=1, source_target_pairs={{0,8},{8,16},{16,24},{1,9},{9,17},{17,25},{2,10},{10,18},{18,26},{... | collective-permute-start | bytes 1572872 | tf_op jit(solution)/shard_map/ppermute | solution.py:421
  109.3 9.3 %collective-permute-start.6 = (bf16[1,256,512]{2,1,0:T(8,128)(2,1)}, bf16[1,256,512]{2,1,0:T(8,128)(2,1)S(1)}, u32[]{:S(2)}, u32[]{:S(2)}) collective-permute-start(bf16[1,256,512]{2,1,0:T(8,128)(2,1)} %get-tuple-element.32), channel_id=1, source_target_pairs={{0,7},{1,6},{2,5},{3,4},{4,3},{5,2},{6,1},{7,0},{8,15},{9,14},{10,... | collective-permute-start | bytes 786440 | tf_op jit(solution)/shard_map/ppermute | solution.py:375
  118.6 42.5 %collective-permute-start.24 = (bf16[3,512,128]{2,1,0:T(8,128)(2,1)S(1)}, bf16[3,512,128]{2,1,0:T(8,128)(2,1)S(1)}, u32[]{:S(2)}, u32[]{:S(2)}) collective-permute-start(bf16[3,512,128]{2,1,0:T(8,128)(2,1)S(1)} %renorm.1.rest_2_), channel_id=1, source_target_pairs={{0,8},{8,16},{16,24},{24,0},{1,9},{9,17},{17,25},{25,1},{2,10},{10... | collective-permute-start | bytes 1179656 | tf_op jit(solution)/shard_map/ppermute | solution.py:397
  121.0 21.3 %copy-start.31 = (bf16[2,256,512]{2,1,0:T(8,128)(2,1)}, bf16[2,256,512]{2,1,0:T(8,128)(2,1)S(1)}, u32[]{:S(2)}) copy-start(bf16[2,256,512]{2,1,0:T(8,128)(2,1)S(1)} %collective-permute-done.14.rest_16_) | copy-start | bytes 1572868
  121.0 64.1 %collective-permute-start.25 = (bf16[3,512,128]{2,1,0:T(8,128)(2,1)S(1)}, bf16[3,512,128]{2,1,0:T(8,128)(2,1)S(1)}, u32[]{:S(2)}, u32[]{:S(2)}) collective-permute-start(bf16[3,512,128]{2,1,0:T(8,128)(2,1)S(1)} %renorm.1.rest_2_), channel_id=1, source_target_pairs={{0,16},{8,24},{16,0},{24,8},{1,17},{9,25},{17,1},{25,9},{2,18},{10... | collective-permute-start | bytes 1179656 | tf_op jit(solution)/shard_map/ppermute | solution.py:397
  123.5 61.6 %collective-permute-start.26 = (bf16[3,512,128]{2,1,0:T(8,128)(2,1)S(1)}, bf16[3,512,128]{2,1,0:T(8,128)(2,1)S(1)}, u32[]{:S(2)}, u32[]{:S(2)}) collective-permute-start(bf16[3,512,128]{2,1,0:T(8,128)(2,1)S(1)} %renorm.1.rest_2_), channel_id=1, source_target_pairs={{0,24},{8,0},{16,8},{24,16},{1,25},{9,1},{17,9},{25,17},{2,26},{10... | collective-permute-start | bytes 1179656 | tf_op jit(solution)/shard_map/ppermute | solution.py:397
  142.3 42.8 %copy-start.17 = (bf16[1,256,512]{2,1,0:T(8,128)(2,1)S(1)}, bf16[1,256,512]{2,1,0:T(8,128)(2,1)}, u32[]{:S(2)}) copy-start(bf16[1,256,512]{2,1,0:T(8,128)(2,1)} %copy-done.16) | copy-start | bytes 786436
  142.3 42.8 %copy-start.19 = (bf16[1,256,512]{2,1,0:T(8,128)(2,1)S(1)}, bf16[1,256,512]{2,1,0:T(8,128)(2,1)}, u32[]{:S(2)}) copy-start(bf16[1,256,512]{2,1,0:T(8,128)(2,1)} %copy-done.18) | copy-start | bytes 786436
  161.1 28.1 %copy-start.9 = (bf16[1,256,512]{2,1,0:T(8,128)(2,1)S(1)}, bf16[1,256,512]{2,1,0:T(8,128)(2,1)}, u32[]{:S(2)}) copy-start(bf16[1,256,512]{2,1,0:T(8,128)(2,1)} %copy-done.8) | copy-start | bytes 786436
  161.1 28.1 %copy-start.11 = (bf16[1,256,512]{2,1,0:T(8,128)(2,1)S(1)}, bf16[1,256,512]{2,1,0:T(8,128)(2,1)}, u32[]{:S(2)}) copy-start(bf16[1,256,512]{2,1,0:T(8,128)(2,1)} %copy-done.10) | copy-start | bytes 786436
  188.2 15.4 %collective-permute-start.28 = (bf16[512,512]{1,0:T(8,128)(2,1)S(1)}, bf16[512,512]{1,0:T(8,128)(2,1)S(1)}, u32[]{:S(2)}, u32[]{:S(2)}) collective-permute-start(bf16[512,512]{1,0:T(8,128)(2,1)S(1)} %readout.5), channel_id=1, source_target_pairs={{0,6},{2,4},{4,2},{6,0},{1,7},{3,5},{5,3},{7,1},{8,14},{10,12},{12... | collective-permute-start | bytes 1572872 | tf_op jit(solution)/shard_map/ppermute | solution.py:394
  192.3 8.5 %collective-permute-start.29 = (bf16[512,512]{1,0:T(8,128)(2,1)S(1)}, bf16[512,512]{1,0:T(8,128)(2,1)}, u32[]{:S(2)}, u32[]{:S(2)}) collective-permute-start(bf16[512,512]{1,0:T(8,128)(2,1)S(1)} %readout.7), channel_id=1, source_target_pairs={{0,2},{2,0},{4,6},{6,4},{1,3},{3,1},{5,7},{7,5},{8,10},{10,8},{12,... | collective-permute-start | bytes 1572872 | tf_op jit(solution)/shard_map/ppermute | solution.py:394
  196.0 17.7 %collective-permute-start.27 = (bf16[512,512]{1,0:T(8,128)(2,1)S(1)}, bf16[512,512]{1,0:T(8,128)(2,1)S(1)}, u32[]{:S(2)}, u32[]{:S(2)}) collective-permute-start(bf16[512,512]{1,0:T(8,128)(2,1)S(1)} %readout.4), channel_id=1, source_target_pairs={{0,4},{2,6},{4,0},{6,2},{1,5},{3,7},{5,1},{7,3},{8,12},{10,14},{12... | collective-permute-start | bytes 1572872 | tf_op jit(solution)/shard_map/ppermute | solution.py:394
  (21 other events, 100.7 us)

commit v2 on v1

--- a/solution.py
+++ b/solution.py
@@ -129,7 +129,7 @@
         ),
         input_output_aliases=aliases,
         compiler_params=pltpu.CompilerParams(
-            dimension_semantics=("arbitrary",), vmem_limit_bytes=40 << 20
+            dimension_semantics=("arbitrary",), vmem_limit_bytes=24 << 20
         ),
         cost_estimate=pl.CostEstimate(
             flops=pairs * AHD * 4, transcendentals=pairs, bytes_accessed=tokens * width * 14
@@ -140,12 +140,18 @@
 
 def update_body(which, rate_ref, *rest, overs, before, parts):
     count = len(overs)
-    pieces, matrices = rest[:count], rest[count : count + 3]
-    outs, steps = rest[count + 3 + before :], rest[-1]
+    pieces = rest[:count]
     if before:
-        outs = outs[:-1]
+        sums_ref, matrices = rest[count : count + 2]
+        *outs, steps, sem = rest[count + 2 :]
+        sums_copy = pltpu.make_async_copy(sums_ref, steps, sem)
+        sums_copy.start()
+    else:
+        steps, matrices = rest[count + 3 :]
+        for at in range(3):
+            matrices[at] = rest[count + at][0].astype(bf16)
     rows = pieces[0].shape[1]
-    gate, up, down = (matrix[...] for matrix in matrices)
+    gate, up, down = (matrices[at] for at in range(3))
     together = max(1, min(ROWS // rows, count))
 
     def joined(arrays):
@@ -166,11 +172,11 @@
         hidden = (silu * pre_up).astype(bf16)
         grad_up = (back * silu).astype(bf16)
         grad_gate = (back * pre_up * (sigma * (1.0 + pre_gate * (1.0 - sigma)))).astype(bf16)
+        if before and not first:
+            sums_copy.wait()
         for at, step in enumerate((dot(key, grad_gate, TN), dot(key, grad_up, TN), dot(hidden, target, TN))):
-            if first:
+            if first or before:
                 steps[at] += step
-            elif before:
-                steps[at] = rest[count + 3][at] + step
             else:
                 steps[at] = step
     if parts == 1:
@@ -182,34 +188,36 @@
             out_ref[...] = steps[:, :, pl.ds(pl.multiple_of(at, wide), wide)].astype(out_ref.dtype)
 
 
-def update_call(which, overs, pieces, rate, matrices, earlier, parts):
+def update_call(which, overs, pieces, rate, given, parts):
     tokens = len(pieces) * pieces[0].shape[1]
     shape = (3, FD, FD // max(parts, 1))
     if parts:
         out_shape = [jax.ShapeDtypeStruct(shape, bf16 if ahead else f32) for ahead in range(parts)]
-        scratch = [pltpu.VMEM((3, FD, FD), f32)]
+        scratch = [pltpu.VMEM((3, FD, FD), f32), pltpu.SemaphoreType.DMA(())]
+        given_specs = [pl.BlockSpec(memory_space=pltpu.HBM), LOCAL]
     else:
-        out_shape = [jax.ShapeDtypeStruct(shape, f32)]
+        out_shape = [jax.ShapeDtypeStruct(shape, f32), jax.ShapeDtypeStruct(shape, bf16)]
         scratch = []
-    args = [rate, *pieces, *matrices, *earlier]
-    return pl.pallas_call(
-        functools.partial(update_body, overs=overs, before=len(earlier), parts=parts),
+        given_specs = [pl.BlockSpec((1, FD, FD), lambda i, w: (w[0], 0, 0))] * 3
+        given = [in_hbm(matrix) for matrix in given]
+    return pl.pallas_call(
+        functools.partial(update_body, overs=overs, before=bool(parts), parts=parts),
         out_shape=out_shape,
         grid_spec=pltpu.PrefetchScalarGridSpec(
             num_scalar_prefetch=1,
             grid=(1,),
-            in_specs=[LOCAL] * len(args),
+            in_specs=[LOCAL] * (1 + len(pieces)) + given_specs,
             out_specs=[LOCAL] * len(out_shape),
             scratch_shapes=scratch,
         ),
         compiler_params=pltpu.CompilerParams(
-            dimension_semantics=("arbitrary",), vmem_limit_bytes=52 << 20
+            dimension_semantics=("arbitrary",), vmem_limit_bytes=30 << 20
         ),
         cost_estimate=pl.CostEstimate(
             flops=tokens * FD * FD * 12, transcendentals=tokens * FD, bytes_accessed=tokens * FD * 4 + FD * FD * 18
         ),
         name="update",
-    )(which, *args)
+    )(which, rate, *pieces, *given)
 
 
 def in_hbm(value):
@@ -242,7 +250,7 @@
             in_specs=[matrix] * 3 + [piece] * len(got),
             out_specs=piece,
         ),
-        compiler_params=pltpu.CompilerParams(vmem_limit_bytes=32 << 20),
+        compiler_params=pltpu.CompilerParams(vmem_limit_bytes=16 << 20),
         cost_estimate=pl.CostEstimate(flops=FD * wide * 3 * 12, transcendentals=0, bytes_accessed=FD * wide * 3 * 20),
         name="renorm",
     )(which, in_hbm(gate), in_hbm(up), in_hbm(down), *got)
@@ -288,35 +296,35 @@
             scratch_shapes=[pltpu.VMEM((3, FD, FD), bf16)],
         ),
         compiler_params=pltpu.CompilerParams(
-            dimension_semantics=("arbitrary",), vmem_limit_bytes=40 << 20
+            dimension_semantics=("arbitrary",), vmem_limit_bytes=16 << 20
         ),
         cost_estimate=pl.CostEstimate(
             flops=rows * FD * FD * 6, transcendentals=rows * FD, bytes_accessed=rows * FD * 8 + FD * FD * 6
         ),
         name="readout",
-    )(which, block, gain, in_hbm(attended), *queries, *pieces)
-
-
-def spread_body(which, *rest, kinds, halves, subs):
+    )(which, block, gain, attended, *queries, *pieces)
+
+
+def spread_body(which, *rest, overs, kinds, halves, subs):
     arrays, outs, sems = rest[:kinds], rest[kinds:-1], rest[-1]
     copies = []
-    for over, out_ref in enumerate(outs):
+    for number, (over, out_ref) in enumerate(zip(overs, outs)):
         target = lax.bitwise_xor(which[2], over)
         at = pl.multiple_of((lax.rem(target, halves) * subs + lax.div(target, halves)) * FD, FD)
         for kind, array in enumerate(arrays):
             copies.append(
-                pltpu.make_async_copy(array.at[:, pl.ds(at, FD)], out_ref.at[kind], sems.at[kind, over])
+                pltpu.make_async_copy(array.at[:, pl.ds(at, FD)], out_ref.at[kind], sems.at[kind, number])
             )
             copies[-1].start()
     for copy in copies:
         copy.wait()
 
 
-def spread_call(which, arrays, halves, subs):
-    count, kinds = halves * subs, len(arrays)
+def spread_call(which, arrays, overs, halves, subs):
+    count, kinds = len(overs), len(arrays)
     shape = (kinds, arrays[0].shape[0], FD)
     return pl.pallas_call(
-        functools.partial(spread_body, kinds=kinds, halves=halves, subs=subs),
+        functools.partial(spread_body, overs=overs, kinds=kinds, halves=halves, subs=subs),
         out_shape=[jax.ShapeDtypeStruct(shape, bf16)] * count,
         grid_spec=pltpu.PrefetchScalarGridSpec(
             num_scalar_prefetch=1,
@@ -325,11 +333,12 @@
             out_specs=[LOCAL] * count,
             scratch_shapes=[pltpu.SemaphoreType.DMA((kinds, count))],
         ),
+        compiler_params=pltpu.CompilerParams(vmem_limit_bytes=12 << 20),
         cost_estimate=pl.CostEstimate(
             flops=count * math.prod(shape), transcendentals=0, bytes_accessed=count * math.prod(shape) * 4
         ),
         name="spread",
-    )(which, *arrays)
+    )(which, *(in_hbm(array) for array in arrays))
 
 
 def arrange_body(which, *rest):
@@ -374,8 +383,13 @@
         links = [(source, source ^ over) for source in range(members)]
         return lax.ppermute(piece, ("sub", "head"), links)
 
-    def spread(arrays):
-        return list(spread_call(which, arrays, halves, subs))
+    def spread(arrays, calls):
+        result = [None] * members
+        for call in range(calls):
+            overs = [over for over in range(members) if over % top * calls // top == call]
+            for over, piece in zip(overs, spread_call(which, arrays, overs, halves, subs)):
+                result[over] = piece
+        return result
 
     def from_earlier(value):
         size = value.shape[0]
@@ -405,10 +419,10 @@
     rate = jnp.concatenate([lax.dynamic_index_in_dim(slots, sub ^ at, 0, keepdims=False) for at in range(subs)])
     rate = rate.reshape(tokens, 1)
 
-    pieces = spread([keys, values])
+    pieces = spread([keys, values], top)
     for over in order:
         pieces[over] = sent(pieces[over], over)
-    query_pieces = spread([queries])
+    query_pieces = spread([queries], 1)
     for over in order:
         query_pieces[over] = sent(query_pieces[over], over)
 
@@ -421,17 +435,13 @@
             early.append(lax.ppermute(late, "grp", links))
 
     parts = groups if FD % (groups * 128) == 0 else 1
-    matrices = [
-        lax.dynamic_index_in_dim(matrix, sub, 0, keepdims=False).astype(bf16)
-        for matrix in (fast_gate, fast_up, fast_down)
-    ]
     last = [over for over in range(members) if over % top == top - 1]
     most = [over for over in range(members) if over % top != top - 1]
 
-    def updated(overs, earlier, parts):
-        return update_call(which, overs, [pieces[over] for over in overs], rate, matrices, earlier, parts)
-
-    begun = updated(most, [], 0)
+    def updated(overs, given, parts):
+        return update_call(which, overs, [pieces[over] for over in overs], rate, given, parts)
+
+    begun = updated(most, (fast_gate, fast_up, fast_down), 0)
     steps = updated(last, begun, parts)
 
     if parts > 1:
@@ -493,6 +503,7 @@
             scratch_shapes=[pltpu.SemaphoreType.DMA((len(slots),))],
         ),
         input_output_aliases={} if out is None else {1 + len(slots): 0},
+        compiler_params=pltpu.CompilerParams(vmem_limit_bytes=6 << 20),
         name="join",
     )(which, *given)
 

time: 218 us -> 215 us (0.986)
  the two profiles are of different devices: /device:TPU:24 before, /device:TPU:25 now
where the time goes in v2:
time: 215 us; the launch traced here: 214 us
  waiting for transfers between devices  97.2 us (45%)
  Pallas kernels  63.6 us (30%)
  starting transfers between devices  32.1 us (15%)
  local copies, waits for them, and re-layouts  14.7 us (7%)
  other arithmetic  6.05 us (3%)
    ppermute x6, waiting for transfers between devices, to_group(): lax.ppermute(value, 'grp', [(source, (source + ahead) % groups) for sourc...  47.2 us
    ppermute x14, waiting for transfers between devices, sent(): return lax.ppermute(piece, ('sub', 'head'), links)  29.2 us
    pallas_call x2, Pallas kernels, attention_call(): pl.pallas_call(functools.partial(attention_body, run=run, early=len(early...  25.8 us
    ppermute x6, waiting for transfers between devices, to_sub(): lax.ppermute(value, 'sub', [(source, source ^ over) for source in range(s...  14.7 us
    ppermute x14, starting transfers between devices, sent(): return lax.ppermute(piece, ('sub', 'head'), links)  13.1 us
    pallas_call x2, Pallas kernels, update_call(): pl.pallas_call(functools.partial(update_body, overs=overs, before=bool(pa...  12.8 us
    unnamed x86, local copies, waits for them, and re-layouts  12.5 us
    pallas_call x5, Pallas kernels, spread_call(): pl.pallas_call(functools.partial(spread_body, overs=overs, kinds=kinds, h...  11.2 us
  transfers between devices with their start and end apart: 30, of which 11 were waited for; matrix products, arithmetic and copies ran while one was open for 4% of the time, Pallas kernels for 27%

profile of v2, /device:TPU:25, one launch (start us, length us, event | category | flops | bytes accessed | tf_op | source)
XLA Modules:
  0.0 214.4 jit_solution(6126340944540221997)
XLA Ops:
  0.1 2.6 %spread.7 = (bf16[2,256,512]{2,1,0:T(8,128)(2,1)S(1)}, bf16[2,256,512]{2,1,0:T(8,128)(2,1)}) custom-call(s32[3]{0:T(128)S(1)} %pad_add_fusion.which, bf16[256,4096]{1,0:T(8,128)(2,1)} %rest_0_.9, bf16[256,4096]{1,0:T(8,128)(2,1)} %rest_1_.7), custom_call_target="tpu_custom_call" | custom-call | flops 524288 | bytes 2097152 | tf_op jit(solution)/shard_map/spread/pallas_call | solution.py:326
  2.7 1.3 collective-permute-start.7
  4.0 1.8 spread.6
  5.9 1.3 collective-permute-start.10
  7.2 1.5 collective-permute-start.20
  8.7 1.2 collective-permute-start.19
  9.9 2.8 %spread.8 = (bf16[2,256,512]{2,1,0:T(8,128)(2,1)}, bf16[2,256,512]{2,1,0:T(8,128)(2,1)}) custom-call(s32[3]{0:T(128)S(1)} %pad_add_fusion.which, bf16[256,4096]{1,0:T(8,128)(2,1)} %rest_0_.9, bf16[256,4096]{1,0:T(8,128)(2,1)} %rest_1_.7), custom_call_target="tpu_custom_call" | custom-call | flops 524288 | bytes 2097152 | tf_op jit(solution)/shard_map/spread/pallas_call | solution.py:326
  12.7 1.8 spread.9
  16.1 2.1 spread.5
  23.8 1.4 collective-permute-start.12
  25.3 1.3 copy.13.rate_ref
  26.7 1.5 collective-permute-start.9
  29.4 1.4 collective-permute-start
  30.8 7.6 %collective-permute-done.11.rest_13_.rest_4_ = bf16[2,256,512]{2,1,0:T(8,128)(2,1)} collective-permute-done((bf16[2,256,512]{2,1,0:T(8,128)(2,1)}, bf16[2,256,512]{2,1,0:T(8,128)(2,1)}, u32[]{:S(2)}, u32[]{:S(2)}) %collective-permute-start.11) | collective-permute-done | bytes 524320 | tf_op jit(solution)/shard_map/ppermute | solution.py:384
  38.5 1.5 collective-permute-start.1
  39.9 9.6 %collective-permute-done.12.rest_14_.rest_5_ = bf16[2,256,512]{2,1,0:T(8,128)(2,1)} collective-permute-done((bf16[2,256,512]{2,1,0:T(8,128)(2,1)}, bf16[2,256,512]{2,1,0:T(8,128)(2,1)}, u32[]{:S(2)}, u32[]{:S(2)}) %collective-permute-start.12) | collective-permute-done | bytes 524320 | tf_op jit(solution)/shard_map/ppermute | solution.py:384
  50.3 1.2 copy-done.6
  51.5 9.0 %update.2 = (f32[3,512,512]{2,1,0:T(8,128)S(1)}, bf16[3,512,512]{2,1,0:T(8,128)(2,1)S(1)}) custom-call(s32[3]{0:T(128)S(1)} %pad_add_fusion.which, f32[2048,1]{1,0:T(8,128)S(1)} %copy-done.6, bf16[2,256,512]{2,1,0:T(8,128)(2,1)S(1)} %get-tuple-element.35.rest_8_.rest_0_, bf16[2,256,512]{2,1,0:T(8,128)(2,1)S(1)} %collective-permute-done.7.rest_9_.rest_1_, ...), custom_call_target="tpu_custom_call" | custom-call | flops 4831838208 | bytes 7864320 | tf_op jit(solution)/shard_map/update/pallas_call | solution.py:203
  61.2 1.4 collective-permute-start.4
  62.6 3.7 %update.3 = (f32[3,512,128]{2,1,0:T(8,128)S(1)}, bf16[3,512,128]{2,1,0:T(8,128)(2,1)S(1)}, bf16[3,512,128]{2,1,0:T(8,128)(2,1)S(1)}, bf16[3,512,128]{2,1,0:T(8,128)(2,1)S(1)}) custom-call(s32[3]{0:T(128)S(1)} %pad_add_fusion.which, f32[2048,1]{1,0:T(8,128)S(1)} %copy-done.7, bf16[2,256,512]{2,1,0:T(8,128)(2,1)S(1)} %collective-permute-done.9.rest_11_.rest_0_, ...), custom_call_target="tpu_custom_call" | custom-call | flops 1610612736 | bytes 5767168 | tf_op jit(solution)/shard_map/update/pallas_call | solution.py:203
  66.3 2.2 %broadcast_select_fusion.2 = bf16[2,256,512]{2,1,0:T(8,128)(2,1)} fusion(bf16[2,256,512]{2,1,0:T(8,128)(2,1)S(1)} %collective-permute-done.7.rest_9_.rest_1_, bf16[2,256,512]{2,1,0:T(8,128)(2,1)} %collective-permute-done.11.rest_13_.rest_4_, pred[]{:T(512)S(6)} %ge.2), kind=kLoop, calls=%fused_computation.2 | loop fusion | flops 262144 | bytes 1572865 | tf_op jit(solution)/shard_map/jit(_where)/select_n | solution.py:434
  68.7 9.5 %collective-permute-done.2.rest_3_.rest_1_ = bf16[1,256,512]{2,1,0:T(8,128)(2,1)S(1)} collective-permute-done((bf16[1,256,512]{2,1,0:T(8,128)(2,1)}, bf16[1,256,512]{2,1,0:T(8,128)(2,1)S(1)}, u32[]{:S(2)}, u32[]{:S(2)}) %collective-permute-start.2) | collective-permute-done | bytes 262176 | tf_op jit(solution)/shard_map/ppermute | solution.py:384
  78.4 2.0 broadcast_select_fusion.1
  80.4 1.3 collective-permute-start.14
  81.7 1.3 collective-permute-start.15
  83.9 1.3 collective-permute-start.16
  85.2 21.7 %collective-permute-done.22.rest_2_ = bf16[3,512,128]{2,1,0:T(8,128)(2,1)S(1)} collective-permute-done((bf16[3,512,128]{2,1,0:T(8,128)(2,1)S(1)}, bf16[3,512,128]{2,1,0:T(8,128)(2,1)S(1)}, u32[]{:S(2)}, u32[]{:S(2)}) %collective-permute-start.22) | collective-permute-done | bytes 393248 | tf_op jit(solution)/shard_map/ppermute | solution.py:411
  107.7 1.3 collective-permute-start.17
  114.8 2.1 renorm.1.rest_2_
  116.9 2.3 %collective-permute-done.6.rest_7_.rest_1_ = bf16[1,256,512]{2,1,0:T(8,128)(2,1)S(1)} collective-permute-done((bf16[1,256,512]{2,1,0:T(8,128)(2,1)S(1)}, bf16[1,256,512]{2,1,0:T(8,128)(2,1)S(1)}, u32[]{:S(2)}, u32[]{:S(2)}) %collective-permute-start.6) | collective-permute-done | bytes 262176 | tf_op jit(solution)/shard_map/ppermute | solution.py:384
  119.2 2.0 collective-permute-start.24
  121.2 1.4 collective-permute-start.25
  122.7 1.7 collective-permute-done.15.rest_17_
  124.4 5.4 %collective-permute-start.26 = (bf16[3,512,128]{2,1,0:T(8,128)(2,1)S(1)}, bf16[3,512,128]{2,1,0:T(8,128)(2,1)S(1)}, u32[]{:S(2)}, u32[]{:S(2)}) collective-permute-start(bf16[3,512,128]{2,1,0:T(8,128)(2,1)S(1)} %renorm.1.rest_2_), channel_id=1, source_target_pairs={{0,24},{8,0},{16,8},{24,16},{1,25},{9,1},{17,9},{25,17},{2,26},{10... | collective-permute-start | bytes 1179656 | tf_op jit(solution)/shard_map/ppermute | solution.py:411
  129.8 12.7 %attention.2.rest_20_ = f32[2048,512]{1,0:T(8,128)S(1)} custom-call(s32[3]{0:T(128)S(1)} %pad_add_fusion.which, bf16[1,256,512]{2,1,0:T(8,128)(2,1)} %copy-done.8, bf16[1,256,512]{2,1,0:T(8,128)(2,1)} %copy-done.10, bf16[1,256,512]{2,1,0:T(8,128)(2,1)} %copy-done.12, bf16[1,256,512]{2,1,0:T(8,128)(2,1)} %copy-done.14, bf16[1,256,512]{2,1,0:T(8,128)(2,1)} %copy-done.16, ...), custom_call_target="tpu_custom_call" | custom-call | flops 2684354560 | bytes 14680064 | tf_op jit(solution)/shard_map/attention/pallas_call | solution.py:114
  142.5 4.3 %collective-permute-done.17.rest_19_ = bf16[2,256,512]{2,1,0:T(8,128)(2,1)} collective-permute-done((bf16[2,256,512]{2,1,0:T(8,128)(2,1)}, bf16[2,256,512]{2,1,0:T(8,128)(2,1)}, u32[]{:S(2)}, u32[]{:S(2)}) %collective-permute-start.17) | collective-permute-done | bytes 524320 | tf_op jit(solution)/shard_map/ppermute | solution.py:435
  146.8 13.1 %attention.3.attended_ref = f32[2048,512]{1,0:T(8,128)S(1)} custom-call(s32[3]{0:T(128)S(1)} %pad_add_fusion.which, bf16[1,256,512]{2,1,0:T(8,128)(2,1)} %copy-done.8, bf16[1,256,512]{2,1,0:T(8,128)(2,1)} %copy-done.10, bf16[1,256,512]{2,1,0:T(8,128)(2,1)} %copy-done.12, bf16[1,256,512]{2,1,0:T(8,128)(2,1)} %copy-done.14, ...), custom_call_target="tpu_custom_call", output_to_operand_aliasing={{}: (21, {})} | custom-call | flops 2684354560 | bytes 14680064 | tf_op jit(solution)/shard_map/attention/pallas_call | solution.py:114
  160.0 25.5 %collective-permute-done.25.rest_4_ = bf16[3,512,128]{2,1,0:T(8,128)(2,1)S(1)} collective-permute-done((bf16[3,512,128]{2,1,0:T(8,128)(2,1)S(1)}, bf16[3,512,128]{2,1,0:T(8,128)(2,1)S(1)}, u32[]{:S(2)}, u32[]{:S(2)}) %collective-permute-start.25) | collective-permute-done | bytes 393248 | tf_op jit(solution)/shard_map/ppermute | solution.py:411
  185.6 1.9 readout.5
  188.2 1.9 readout.7
  190.2 1.9 readout.4
  192.1 1.3 collective-permute-start.27
  193.3 1.9 readout.6.rest_0_
  195.3 1.5 join.3.rest_1_
  196.8 5.0 %collective-permute-done.28.rest_0_ = bf16[512,512]{1,0:T(8,128)(2,1)S(1)} collective-permute-done((bf16[512,512]{1,0:T(8,128)(2,1)S(1)}, bf16[512,512]{1,0:T(8,128)(2,1)S(1)}, u32[]{:S(2)}, u32[]{:S(2)}) %collective-permute-start.28) | collective-permute-done | bytes 524320 | tf_op jit(solution)/shard_map/ppermute | solution.py:408
  201.8 1.3 join.4.rest_1_
  203.1 9.7 %collective-permute-done.27.rest_0_ = bf16[512,512]{1,0:T(8,128)(2,1)S(1)} collective-permute-done((bf16[512,512]{1,0:T(8,128)(2,1)S(1)}, bf16[512,512]{1,0:T(8,128)(2,1)S(1)}, u32[]{:S(2)}, u32[]{:S(2)}) %collective-permute-start.27) | collective-permute-done | bytes 524320 | tf_op jit(solution)/shard_map/ppermute | solution.py:408
  212.9 1.3 join.5
  (126 shorter events, 18.7 us)
Async XLA Ops:
  2.7 24.0 %collective-permute-start.7 = (bf16[2,256,512]{2,1,0:T(8,128)(2,1)S(1)}, bf16[2,256,512]{2,1,0:T(8,128)(2,1)S(1)}, u32[]{:S(2)}, u32[]{:S(2)}) collective-permute-start(bf16[2,256,512]{2,1,0:T(8,128)(2,1)S(1)} %get-tuple-element.36), channel_id=1, source_target_pairs={{0,1},{1,0},{2,3},{3,2},{4,5},{5,4},{6,7},{7,6},{8,9},{9,8},{10,11... | collective-permute-start | bytes 1572872 | tf_op jit(solution)/shard_map/ppermute | solution.py:384
  5.8 44.4 %copy-start.3 = (bf16[2,256,512]{2,1,0:T(8,128)(2,1)}, bf16[2,256,512]{2,1,0:T(8,128)(2,1)S(1)}, u32[]{:S(2)}) copy-start(bf16[2,256,512]{2,1,0:T(8,128)(2,1)S(1)} %get-tuple-element.35.rest_8_.rest_0_) | copy-start | bytes 1572868
  5.9 22.3 %collective-permute-start.10 = (bf16[2,256,512]{2,1,0:T(8,128)(2,1)S(1)}, bf16[2,256,512]{2,1,0:T(8,128)(2,1)S(1)}, u32[]{:S(2)}, u32[]{:S(2)}) collective-permute-start(bf16[2,256,512]{2,1,0:T(8,128)(2,1)S(1)} %get-tuple-element.39), channel_id=1, source_target_pairs={{0,4},{1,5},{2,6},{3,7},{4,0},{5,1},{6,2},{7,3},{8,12},{9,13},{10,... | collective-permute-start | bytes 1572872 | tf_op jit(solution)/shard_map/ppermute | solution.py:384
  7.2 16.1 %collective-permute-start.20 = (f32[512]{0:T(512)S(1)}, f32[512]{0:T(512)S(1)}, u32[]{:S(2)}, u32[]{:S(2)}) collective-permute-start(f32[512]{0:T(512)S(1)} %bitcast.31), channel_id=1, source_target_pairs={{0,6},{2,4},{4,2},{6,0},{1,7},{3,5},{5,3},{7,1},{8,14},{10,12},{12... | collective-permute-start | bytes 6152 | tf_op jit(solution)/shard_map/ppermute | solution.py:408
  8.7 15.1 %collective-permute-start.19 = (f32[512]{0:T(512)S(1)}, f32[512]{0:T(512)S(1)}, u32[]{:S(2)}, u32[]{:S(2)}) collective-permute-start(f32[512]{0:T(512)S(1)} %bitcast.30), channel_id=1, source_target_pairs={{0,4},{2,6},{4,0},{6,2},{1,5},{3,7},{5,1},{7,3},{8,12},{10,14},{12... | collective-permute-start | bytes 6152 | tf_op jit(solution)/shard_map/ppermute | solution.py:408
  9.9 13.9 %collective-permute-start.18 = (f32[512]{0:T(512)S(1)}, f32[512]{0:T(512)S(1)}, u32[]{:S(2)}, u32[]{:S(2)}) collective-permute-start(f32[512]{0:T(512)S(1)} %bitcast.29), channel_id=1, source_target_pairs={{0,2},{2,0},{4,6},{6,4},{1,3},{3,1},{5,7},{7,5},{8,10},{10,8},{12,... | collective-permute-start | bytes 6152 | tf_op jit(solution)/shard_map/ppermute | solution.py:408
  23.3 6.2 %collective-permute-start.8 = (bf16[2,256,512]{2,1,0:T(8,128)(2,1)}, bf16[2,256,512]{2,1,0:T(8,128)(2,1)S(1)}, u32[]{:S(2)}, u32[]{:S(2)}) collective-permute-start(bf16[2,256,512]{2,1,0:T(8,128)(2,1)} %get-tuple-element.37), channel_id=1, source_target_pairs={{0,2},{1,3},{2,0},{3,1},{4,6},{5,7},{6,4},{7,5},{8,10},{9,11},{10,... | collective-permute-start | bytes 1572872 | tf_op jit(solution)/shard_map/ppermute | solution.py:384
  23.8 14.7 %collective-permute-start.11 = (bf16[2,256,512]{2,1,0:T(8,128)(2,1)}, bf16[2,256,512]{2,1,0:T(8,128)(2,1)}, u32[]{:S(2)}, u32[]{:S(2)}) collective-permute-start(bf16[2,256,512]{2,1,0:T(8,128)(2,1)} %get-tuple-element.40), channel_id=1, source_target_pairs={{0,5},{1,4},{2,7},{3,6},{4,1},{5,0},{6,3},{7,2},{8,13},{9,12},{10,... | collective-permute-start | bytes 1572872 | tf_op jit(solution)/shard_map/ppermute | solution.py:384
  23.8 25.7 %collective-permute-start.12 = (bf16[2,256,512]{2,1,0:T(8,128)(2,1)}, bf16[2,256,512]{2,1,0:T(8,128)(2,1)}, u32[]{:S(2)}, u32[]{:S(2)}) collective-permute-start(bf16[2,256,512]{2,1,0:T(8,128)(2,1)} %get-tuple-element.41), channel_id=1, source_target_pairs={{0,6},{1,7},{2,4},{3,5},{4,2},{5,3},{6,0},{7,1},{8,14},{9,15},{10,... | collective-permute-start | bytes 1572872 | tf_op jit(solution)/shard_map/ppermute | solution.py:384
  26.7 39.6 %copy-start.2 = (bf16[2,256,512]{2,1,0:T(8,128)(2,1)}, bf16[2,256,512]{2,1,0:T(8,128)(2,1)S(1)}, u32[]{:S(2)}) copy-start(bf16[2,256,512]{2,1,0:T(8,128)(2,1)S(1)} %collective-permute-done.7.rest_9_.rest_1_) | copy-start | bytes 1572868
  26.7 33.9 %collective-permute-start.9 = (bf16[2,256,512]{2,1,0:T(8,128)(2,1)}, bf16[2,256,512]{2,1,0:T(8,128)(2,1)S(1)}, u32[]{:S(2)}, u32[]{:S(2)}) collective-permute-start(bf16[2,256,512]{2,1,0:T(8,128)(2,1)} %copy-done.31), channel_id=1, source_target_pairs={{0,3},{1,2},{2,1},{3,0},{4,7},{5,6},{6,5},{7,4},{8,11},{9,10},{10,... | collective-permute-start | bytes 1572872 | tf_op jit(solution)/shard_map/ppermute | solution.py:384
  28.1 32.4 %copy-start.4 = (bf16[2,256,512]{2,1,0:T(8,128)(2,1)}, bf16[2,256,512]{2,1,0:T(8,128)(2,1)S(1)}, u32[]{:S(2)}) copy-start(bf16[2,256,512]{2,1,0:T(8,128)(2,1)S(1)} %collective-permute-done.10.rest_12_.rest_3_) | copy-start | bytes 1572868
  28.1 33.0 %collective-permute-start.13 = (bf16[2,256,512]{2,1,0:T(8,128)(2,1)}, bf16[2,256,512]{2,1,0:T(8,128)(2,1)S(1)}, u32[]{:S(2)}, u32[]{:S(2)}) collective-permute-start(bf16[2,256,512]{2,1,0:T(8,128)(2,1)} %copy-done.30), channel_id=1, source_target_pairs={{0,7},{1,6},{2,5},{3,4},{4,3},{5,2},{6,1},{7,0},{8,15},{9,14},{10,... | collective-permute-start | bytes 1572872 | tf_op jit(solution)/shard_map/ppermute | solution.py:384
  29.4 49.0 %copy-start.5 = (bf16[2,256,512]{2,1,0:T(8,128)(2,1)}, bf16[2,256,512]{2,1,0:T(8,128)(2,1)S(1)}, u32[]{:S(2)}) copy-start(bf16[2,256,512]{2,1,0:T(8,128)(2,1)S(1)} %collective-permute-done.8.rest_10_.rest_2_) | copy-start | bytes 1572868
  29.4 39.1 %collective-permute-start = (bf16[1,256,512]{2,1,0:T(8,128)(2,1)}, bf16[1,256,512]{2,1,0:T(8,128)(2,1)S(1)}, u32[]{:S(2)}, u32[]{:S(2)}) collective-permute-start(bf16[1,256,512]{2,1,0:T(8,128)(2,1)} %copy-done.40), channel_id=1, source_target_pairs={{0,1},{1,0},{2,3},{3,2},{4,5},{5,4},{6,7},{7,6},{8,9},{9,8},{10,11... | collective-permute-start | bytes 786440 | tf_op jit(solution)/shard_map/ppermute | solution.py:384
  38.5 30.2 %collective-permute-start.1 = (bf16[1,256,512]{2,1,0:T(8,128)(2,1)}, bf16[1,256,512]{2,1,0:T(8,128)(2,1)S(1)}, u32[]{:S(2)}, u32[]{:S(2)}) collective-permute-start(bf16[1,256,512]{2,1,0:T(8,128)(2,1)} %copy-done.39), channel_id=1, source_target_pairs={{0,2},{1,3},{2,0},{3,1},{4,6},{5,7},{6,4},{7,5},{8,10},{9,11},{10,... | collective-permute-start | bytes 786440 | tf_op jit(solution)/shard_map/ppermute | solution.py:384
  49.5 28.6 %collective-permute-start.2 = (bf16[1,256,512]{2,1,0:T(8,128)(2,1)}, bf16[1,256,512]{2,1,0:T(8,128)(2,1)S(1)}, u32[]{:S(2)}, u32[]{:S(2)}) collective-permute-start(bf16[1,256,512]{2,1,0:T(8,128)(2,1)} %copy-done.38), channel_id=1, source_target_pairs={{0,3},{1,2},{2,1},{3,0},{4,7},{5,6},{6,5},{7,4},{8,11},{9,10},{10,... | collective-permute-start | bytes 786440 | tf_op jit(solution)/shard_map/ppermute | solution.py:384
  51.5 9.7 %copy-start.35 = (bf16[1,256,512]{2,1,0:T(8,128)(2,1)S(1)}, bf16[1,256,512]{2,1,0:T(8,128)(2,1)}, u32[]{:S(2)}) copy-start(bf16[1,256,512]{2,1,0:T(8,128)(2,1)} %copy-done.34) | copy-start | bytes 786436
  51.5 11.1 %copy-start.7 = (f32[2048,1]{1,0:T(8,128)S(1)}, f32[2048,1]{1,0:T(8,128)}, u32[]{:S(2)}) copy-start(f32[2048,1]{1,0:T(8,128)} %copy.13.rate_ref) | copy-start | bytes 24580
  60.5 22.4 %copy-start = (bf16[2,256,512]{2,1,0:T(8,128)(2,1)}, bf16[2,256,512]{2,1,0:T(8,128)(2,1)S(1)}, u32[]{:S(2)}) copy-start(bf16[2,256,512]{2,1,0:T(8,128)(2,1)S(1)} %collective-permute-done.9.rest_11_.rest_0_) | copy-start | bytes 1572868
  60.6 17.7 %collective-permute-start.3 = (bf16[1,256,512]{2,1,0:T(8,128)(2,1)S(1)}, bf16[1,256,512]{2,1,0:T(8,128)(2,1)S(1)}, u32[]{:S(2)}, u32[]{:S(2)}) collective-permute-start(bf16[1,256,512]{2,1,0:T(8,128)(2,1)S(1)} %copy-done.37), channel_id=1, source_target_pairs={{0,4},{1,5},{2,6},{3,7},{4,0},{5,1},{6,2},{7,3},{8,12},{9,13},{10,... | collective-permute-start | bytes 786440 | tf_op jit(solution)/shard_map/ppermute | solution.py:384
  61.2 21.8 %copy-start.1 = (bf16[2,256,512]{2,1,0:T(8,128)(2,1)}, bf16[2,256,512]{2,1,0:T(8,128)(2,1)S(1)}, u32[]{:S(2)}) copy-start(bf16[2,256,512]{2,1,0:T(8,128)(2,1)S(1)} %collective-permute-done.13.rest_15_.rest_1_) | copy-start | bytes 1572868
  61.2 19.2 %collective-permute-start.4 = (bf16[1,256,512]{2,1,0:T(8,128)(2,1)S(1)}, bf16[1,256,512]{2,1,0:T(8,128)(2,1)S(1)}, u32[]{:S(2)}, u32[]{:S(2)}) collective-permute-start(bf16[1,256,512]{2,1,0:T(8,128)(2,1)S(1)} %copy-done.35), channel_id=1, source_target_pairs={{0,5},{1,4},{2,7},{3,6},{4,1},{5,0},{6,3},{7,2},{8,13},{9,12},{10,... | collective-permute-start | bytes 786440 | tf_op jit(solution)/shard_map/ppermute | solution.py:384
  66.3 17.6 %copy-start.24 = (f32[3,512,128]{2,1,0:T(8,128)}, f32[3,512,128]{2,1,0:T(8,128)S(1)}, u32[]{:S(2)}) copy-start(f32[3,512,128]{2,1,0:T(8,128)S(1)} %get-tuple-element.45.rest_0_) | copy-start | bytes 2359300
  68.5 48.4 %copy-start.10 = (bf16[1,256,512]{2,1,0:T(8,128)(2,1)}, bf16[1,256,512]{2,1,0:T(8,128)(2,1)S(1)}, u32[]{:S(2)}) copy-start(bf16[1,256,512]{2,1,0:T(8,128)(2,1)S(1)} %collective-permute-done.rest_1_) | copy-start | bytes 786436
  68.5 13.1 %collective-permute-start.5 = (bf16[1,256,512]{2,1,0:T(8,128)(2,1)S(1)}, bf16[1,256,512]{2,1,0:T(8,128)(2,1)S(1)}, u32[]{:S(2)}, u32[]{:S(2)}) collective-permute-start(bf16[1,256,512]{2,1,0:T(8,128)(2,1)S(1)} %copy-done.33), channel_id=1, source_target_pairs={{0,6},{1,7},{2,4},{3,5},{4,2},{5,3},{6,0},{7,1},{8,14},{9,15},{10,... | collective-permute-start | bytes 786440 | tf_op jit(solution)/shard_map/ppermute | solution.py:384
  68.6 15.3 %copy-start.12 = (bf16[1,256,512]{2,1,0:T(8,128)(2,1)}, bf16[1,256,512]{2,1,0:T(8,128)(2,1)S(1)}, u32[]{:S(2)}) copy-start(bf16[1,256,512]{2,1,0:T(8,128)(2,1)S(1)} %collective-permute-done.1.rest_2_.rest_0_) | copy-start | bytes 786436
  68.6 15.3 %collective-permute-start.21 = (bf16[3,512,128]{2,1,0:T(8,128)(2,1)S(1)}, bf16[3,512,128]{2,1,0:T(8,128)(2,1)S(1)}, u32[]{:S(2)}, u32[]{:S(2)}) collective-permute-start(bf16[3,512,128]{2,1,0:T(8,128)(2,1)S(1)} %get-tuple-element.46), channel_id=1, source_target_pairs={{0,8},{8,16},{16,24},{24,0},{1,9},{9,17},{17,25},{25,1},{2,10},{10... | collective-permute-start | bytes 1179656 | tf_op jit(solution)/shard_map/ppermute | solution.py:411
  78.2 28.7 %collective-permute-start.22 = (bf16[3,512,128]{2,1,0:T(8,128)(2,1)S(1)}, bf16[3,512,128]{2,1,0:T(8,128)(2,1)S(1)}, u32[]{:S(2)}, u32[]{:S(2)}) collective-permute-start(bf16[3,512,128]{2,1,0:T(8,128)(2,1)S(1)} %get-tuple-element.47), channel_id=1, source_target_pairs={{0,16},{8,24},{16,0},{24,8},{1,17},{9,25},{17,1},{25,9},{2,18},{10... | collective-permute-start | bytes 1179656 | tf_op jit(solution)/shard_map/ppermute | solution.py:411
  78.2 38.7 %copy-start.16 = (bf16[1,256,512]{2,1,0:T(8,128)(2,1)}, bf16[1,256,512]{2,1,0:T(8,128)(2,1)S(1)}, u32[]{:S(2)}) copy-start(bf16[1,256,512]{2,1,0:T(8,128)(2,1)S(1)} %collective-permute-done.3.rest_4_.rest_0_) | copy-start | bytes 786436
  78.2 30.7 %collective-permute-start.23 = (bf16[3,512,128]{2,1,0:T(8,128)(2,1)S(1)}, bf16[3,512,128]{2,1,0:T(8,128)(2,1)S(1)}, u32[]{:S(2)}, u32[]{:S(2)}) collective-permute-start(bf16[3,512,128]{2,1,0:T(8,128)(2,1)S(1)} %get-tuple-element.48), channel_id=1, source_target_pairs={{0,24},{8,0},{16,8},{24,16},{1,25},{9,1},{17,9},{25,17},{2,26},{10... | collective-permute-start | bytes 1179656 | tf_op jit(solution)/shard_map/ppermute | solution.py:411
  80.4 36.6 %copy-start.18 = (bf16[1,256,512]{2,1,0:T(8,128)(2,1)}, bf16[1,256,512]{2,1,0:T(8,128)(2,1)S(1)}, u32[]{:S(2)}) copy-start(bf16[1,256,512]{2,1,0:T(8,128)(2,1)S(1)} %collective-permute-done.4.rest_5_.rest_1_) | copy-start | bytes 786436
  80.4 40.9 %collective-permute-start.14 = (bf16[2,256,512]{2,1,0:T(8,128)(2,1)}, bf16[2,256,512]{2,1,0:T(8,128)(2,1)S(1)}, u32[]{:S(2)}, u32[]{:S(2)}) collective-permute-start(bf16[2,256,512]{2,1,0:T(8,128)(2,1)} %broadcast_select_fusion.3), channel_id=1, source_target_pairs={{0,8},{8,16},{16,24},{1,9},{9,17},{17,25},{2,10},{10,18},{18,26},{... | collective-permute-start | bytes 1572872 | tf_op jit(solution)/shard_map/ppermute | solution.py:435
  81.7 35.3 %copy-start.20 = (bf16[1,256,512]{2,1,0:T(8,128)(2,1)}, bf16[1,256,512]{2,1,0:T(8,128)(2,1)S(1)}, u32[]{:S(2)}) copy-start(bf16[1,256,512]{2,1,0:T(8,128)(2,1)S(1)} %collective-permute-done.5.rest_6_.rest_0_) | copy-start | bytes 786436
  81.7 42.7 %collective-permute-start.15 = (bf16[2,256,512]{2,1,0:T(8,128)(2,1)}, bf16[2,256,512]{2,1,0:T(8,128)(2,1)}, u32[]{:S(2)}, u32[]{:S(2)}) collective-permute-start(bf16[2,256,512]{2,1,0:T(8,128)(2,1)} %broadcast_select_fusion.2), channel_id=1, source_target_pairs={{0,8},{8,16},{16,24},{1,9},{9,17},{17,25},{2,10},{10,18},{18,26},{... | collective-permute-start | bytes 1572872 | tf_op jit(solution)/shard_map/ppermute | solution.py:435
  83.9 58.6 %collective-permute-start.16 = (bf16[2,256,512]{2,1,0:T(8,128)(2,1)}, bf16[2,256,512]{2,1,0:T(8,128)(2,1)}, u32[]{:S(2)}, u32[]{:S(2)}) collective-permute-start(bf16[2,256,512]{2,1,0:T(8,128)(2,1)} %broadcast_select_fusion.1), channel_id=1, source_target_pairs={{0,8},{8,16},{16,24},{1,9},{9,17},{17,25},{2,10},{10,18},{18,26},{... | collective-permute-start | bytes 1572872 | tf_op jit(solution)/shard_map/ppermute | solution.py:435
  107.7 39.2 %collective-permute-start.17 = (bf16[2,256,512]{2,1,0:T(8,128)(2,1)}, bf16[2,256,512]{2,1,0:T(8,128)(2,1)}, u32[]{:S(2)}, u32[]{:S(2)}) collective-permute-start(bf16[2,256,512]{2,1,0:T(8,128)(2,1)} %broadcast_select_fusion), channel_id=1, source_target_pairs={{0,8},{8,16},{16,24},{1,9},{9,17},{17,25},{2,10},{10,18},{18,26},{... | collective-permute-start | bytes 1572872 | tf_op jit(solution)/shard_map/ppermute | solution.py:435
  109.7 9.5 %collective-permute-start.6 = (bf16[1,256,512]{2,1,0:T(8,128)(2,1)S(1)}, bf16[1,256,512]{2,1,0:T(8,128)(2,1)S(1)}, u32[]{:S(2)}, u32[]{:S(2)}) collective-permute-start(bf16[1,256,512]{2,1,0:T(8,128)(2,1)S(1)} %get-tuple-element.34), channel_id=1, source_target_pairs={{0,7},{1,6},{2,5},{3,4},{4,3},{5,2},{6,1},{7,0},{8,15},{9,14},{10,... | collective-permute-start | bytes 786440 | tf_op jit(solution)/shard_map/ppermute | solution.py:384
  119.2 10.5 %copy-start.22 = (bf16[1,256,512]{2,1,0:T(8,128)(2,1)}, bf16[1,256,512]{2,1,0:T(8,128)(2,1)S(1)}, u32[]{:S(2)}) copy-start(bf16[1,256,512]{2,1,0:T(8,128)(2,1)S(1)} %collective-permute-done.6.rest_7_.rest_1_) | copy-start | bytes 786436
  119.2 40.8 %collective-permute-start.24 = (bf16[3,512,128]{2,1,0:T(8,128)(2,1)S(1)}, bf16[3,512,128]{2,1,0:T(8,128)(2,1)S(1)}, u32[]{:S(2)}, u32[]{:S(2)}) collective-permute-start(bf16[3,512,128]{2,1,0:T(8,128)(2,1)S(1)} %renorm.1.rest_2_), channel_id=1, source_target_pairs={{0,8},{8,16},{16,24},{24,0},{1,9},{9,17},{17,25},{25,1},{2,10},{10... | collective-permute-start | bytes 1179656 | tf_op jit(solution)/shard_map/ppermute | solution.py:411
  121.2 21.2 %copy-start.41 = (bf16[2,256,512]{2,1,0:T(8,128)(2,1)}, bf16[2,256,512]{2,1,0:T(8,128)(2,1)S(1)}, u32[]{:S(2)}) copy-start(bf16[2,256,512]{2,1,0:T(8,128)(2,1)S(1)} %collective-permute-done.14.rest_16_) | copy-start | bytes 1572868
  121.2 64.3 %collective-permute-start.25 = (bf16[3,512,128]{2,1,0:T(8,128)(2,1)S(1)}, bf16[3,512,128]{2,1,0:T(8,128)(2,1)S(1)}, u32[]{:S(2)}, u32[]{:S(2)}) collective-permute-start(bf16[3,512,128]{2,1,0:T(8,128)(2,1)S(1)} %renorm.1.rest_2_), channel_id=1, source_target_pairs={{0,16},{8,24},{16,0},{24,8},{1,17},{9,25},{17,1},{25,9},{2,18},{10... | collective-permute-start | bytes 1179656 | tf_op jit(solution)/shard_map/ppermute | solution.py:411
  124.4 61.2 %collective-permute-start.26 = (bf16[3,512,128]{2,1,0:T(8,128)(2,1)S(1)}, bf16[3,512,128]{2,1,0:T(8,128)(2,1)S(1)}, u32[]{:S(2)}, u32[]{:S(2)}) collective-permute-start(bf16[3,512,128]{2,1,0:T(8,128)(2,1)S(1)} %renorm.1.rest_2_), channel_id=1, source_target_pairs={{0,24},{8,0},{16,8},{24,16},{1,25},{9,1},{17,9},{25,17},{2,26},{10... | collective-permute-start | bytes 1179656 | tf_op jit(solution)/shard_map/ppermute | solution.py:411
  142.5 43.1 %copy-start.21 = (bf16[1,256,512]{2,1,0:T(8,128)(2,1)S(1)}, bf16[1,256,512]{2,1,0:T(8,128)(2,1)}, u32[]{:S(2)}) copy-start(bf16[1,256,512]{2,1,0:T(8,128)(2,1)} %copy-done.20) | copy-start | bytes 786436
  142.5 43.1 %copy-start.23 = (bf16[1,256,512]{2,1,0:T(8,128)(2,1)S(1)}, bf16[1,256,512]{2,1,0:T(8,128)(2,1)}, u32[]{:S(2)}) copy-start(bf16[1,256,512]{2,1,0:T(8,128)(2,1)} %copy-done.22) | copy-start | bytes 786436
  187.5 14.3 %collective-permute-start.28 = (bf16[512,512]{1,0:T(8,128)(2,1)S(1)}, bf16[512,512]{1,0:T(8,128)(2,1)S(1)}, u32[]{:S(2)}, u32[]{:S(2)}) collective-permute-start(bf16[512,512]{1,0:T(8,128)(2,1)S(1)} %readout.5), channel_id=1, source_target_pairs={{0,6},{2,4},{4,2},{6,0},{1,7},{3,5},{5,3},{7,1},{8,14},{10,12},{12... | collective-permute-start | bytes 1572872 | tf_op jit(solution)/shard_map/ppermute | solution.py:408
  190.1 5.2 %collective-permute-start.29 = (bf16[512,512]{1,0:T(8,128)(2,1)S(1)}, bf16[512,512]{1,0:T(8,128)(2,1)S(1)}, u32[]{:S(2)}, u32[]{:S(2)}) collective-permute-start(bf16[512,512]{1,0:T(8,128)(2,1)S(1)} %readout.7), channel_id=1, source_target_pairs={{0,2},{2,0},{4,6},{6,4},{1,3},{3,1},{5,7},{7,5},{8,10},{10,8},{12,... | collective-permute-start | bytes 1572872 | tf_op jit(solution)/shard_map/ppermute | solution.py:408
  192.1 20.8 %collective-permute-start.27 = (bf16[512,512]{1,0:T(8,128)(2,1)S(1)}, bf16[512,512]{1,0:T(8,128)(2,1)S(1)}, u32[]{:S(2)}, u32[]{:S(2)}) collective-permute-start(bf16[512,512]{1,0:T(8,128)(2,1)S(1)} %readout.4), channel_id=1, source_target_pairs={{0,4},{2,6},{4,0},{6,2},{1,5},{3,7},{5,1},{7,3},{8,12},{10,14},{12... | collective-permute-start | bytes 1572872 | tf_op jit(solution)/shard_map/ppermute | solution.py:408
  (25 other events, 53.2 us)

commit v3 on v2

--- a/solution.py
+++ b/solution.py
@@ -31,6 +31,8 @@
 TN = ((0,), (0,))
 
 LOCAL = pl.BlockSpec(memory_space=pltpu.VMEM)
+
+SHARES = ((0, 2), (2, 3))
 
 
 def attention_body(which, *rest, run, early, block, count):
@@ -183,16 +185,25 @@
         outs[0][...] = steps[...]
     elif parts:
         wide = FD // parts
-        for ahead, out_ref in enumerate(outs):
-            at = lax.rem(which[1] + ahead, parts) * wide
-            out_ref[...] = steps[:, :, pl.ds(pl.multiple_of(at, wide), wide)].astype(out_ref.dtype)
+        for number, (low, high) in enumerate(SHARES):
+            for ahead in range(parts):
+                out_ref = outs[number * parts + ahead]
+                at = lax.rem(which[1] + ahead, parts) * wide
+                out_ref[...] = steps[low:high, :, pl.ds(pl.multiple_of(at, wide), wide)].astype(out_ref.dtype)
 
 
 def update_call(which, overs, pieces, rate, given, parts):
     tokens = len(pieces) * pieces[0].shape[1]
     shape = (3, FD, FD // max(parts, 1))
+    if parts > 1:
+        out_shape = [
+            jax.ShapeDtypeStruct((high - low, *shape[1:]), bf16 if ahead else f32)
+            for low, high in SHARES
+            for ahead in range(parts)
+        ]
+    elif parts:
+        out_shape = [jax.ShapeDtypeStruct(shape, f32)]
     if parts:
-        out_shape = [jax.ShapeDtypeStruct(shape, bf16 if ahead else f32) for ahead in range(parts)]
         scratch = [pltpu.VMEM((3, FD, FD), f32), pltpu.SemaphoreType.DMA(())]
         given_specs = [pl.BlockSpec(memory_space=pltpu.HBM), LOCAL]
     else:
@@ -224,19 +235,20 @@
     return pltpu.with_memory_space_constraint(value, pltpu.HBM)
 
 
-def renorm_body(which, gate_ref, up_ref, down_ref, *rest):
-    *got, out_ref = rest
-    for at, initial_ref in enumerate((gate_ref, up_ref, down_ref)):
+def renorm_body(which, *rest):
+    *refs, out_ref = rest
+    count = out_ref.shape[0]
+    for at, initial_ref in enumerate(refs[:count]):
         initial = initial_ref[0]
         moved = initial
-        for got_ref in got:
+        for got_ref in refs[count:]:
             moved = moved + got_ref[at].astype(f32)
         norm_before = jnp.sqrt(jnp.sum(initial * initial, axis=0, keepdims=True) + epsilon)
         norm_after = jnp.sqrt(jnp.sum(moved * moved, axis=0, keepdims=True) + epsilon)
         out_ref[at] = (moved * (norm_before / norm_after)).astype(bf16)
 
 
-def renorm_call(which, got, gate, up, down):
+def renorm_call(which, got, matrices):
     shape = got[0].shape
     wide = shape[-1]
     matrix = pl.BlockSpec((1, FD, wide), lambda i, w: (w[0], 0, w[1]))
@@ -247,23 +259,28 @@
         grid_spec=pltpu.PrefetchScalarGridSpec(
             num_scalar_prefetch=1,
             grid=(1,),
-            in_specs=[matrix] * 3 + [piece] * len(got),
+            in_specs=[matrix] * len(matrices) + [piece] * len(got),
             out_specs=piece,
         ),
         compiler_params=pltpu.CompilerParams(vmem_limit_bytes=16 << 20),
         cost_estimate=pl.CostEstimate(flops=FD * wide * 3 * 12, transcendentals=0, bytes_accessed=FD * wide * 3 * 20),
         name="renorm",
-    )(which, in_hbm(gate), in_hbm(up), in_hbm(down), *got)
-
-
-def readout_body(which, block, gain_ref, attended_ref, *rest, count):
+    )(which, *(in_hbm(matrix) for matrix in matrices), *got)
+
+
+def readout_body(which, block, gain_ref, attended_ref, *rest, count, shares):
     queries = rest[:count]
     *pieces, out_ref, weights = rest[count:]
     rows = queries[0].shape[1]
-    wide = FD // len(pieces)
-    for back, piece_ref in enumerate(pieces):
-        column = lax.rem(which[1] + len(pieces) - back, len(pieces)) * wide
-        weights[:, :, pl.ds(pl.multiple_of(column, wide), wide)] = piece_ref[...]
+    parts = len(pieces) // shares
+    wide = FD // parts
+    low = 0
+    for number in range(shares):
+        high = low + pieces[number * parts].shape[0]
+        for back in range(parts):
+            column = lax.rem(which[1] + parts - back, parts) * wide
+            weights[low:high, :, pl.ds(pl.multiple_of(column, wide), wide)] = pieces[number * parts + back][...]
+        low = high
     query = queries[0][0] if count == 1 else jnp.concatenate([ref[0] for ref in queries], axis=0)
     gate = dot(query, weights[0], NN)
     up = dot(query, weights[1], NN)
@@ -277,15 +294,16 @@
         out_ref[here, :] = (attended_ref[here, :] + readout[at * rows : (at + 1) * rows]).astype(bf16)
 
 
-def readout_call(which, block, queries, pieces, attended, gain):
+def readout_call(which, block, queries, weights, attended, gain):
     count = len(queries)
+    pieces = [piece for share in weights for piece in share]
     rows = count * queries[0].shape[1]
 
     def whole(array):
         return pl.BlockSpec(array.shape, lambda i, w, b: (0,) * array.ndim)
 
     return pl.pallas_call(
-        functools.partial(readout_body, count=count),
+        functools.partial(readout_body, count=count, shares=len(weights)),
         out_shape=jax.ShapeDtypeStruct((rows, FD), bf16),
         grid_spec=pltpu.PrefetchScalarGridSpec(
             num_scalar_prefetch=2,
@@ -387,6 +405,8 @@
         result = [None] * members
         for call in range(calls):
             overs = [over for over in range(members) if over % top * calls // top == call]
+            if calls > 1 and call < 2:
+                overs = [1 - call, top + call]
             for over, piece in zip(overs, spread_call(which, arrays, overs, halves, subs)):
                 result[over] = piece
         return result
@@ -444,14 +464,18 @@
     begun = updated(most, (fast_gate, fast_up, fast_down), 0)
     steps = updated(last, begun, parts)
 
+    matrices = (fast_gate, fast_up, fast_down)
+    weights = []
     if parts > 1:
-        got = [steps[0]] + [to_group(steps[ahead], ahead) for ahead in range(1, parts)]
-        mine = renorm_call(which, got, fast_gate, fast_up, fast_down)
-        weights = [mine] + [to_group(mine, ahead) for ahead in range(1, parts)]
+        for number, (low, high) in enumerate(SHARES):
+            share = steps[number * parts : (number + 1) * parts]
+            got = [share[0]] + [to_group(share[ahead], ahead) for ahead in range(1, parts)]
+            mine = renorm_call(which, got, matrices[low:high])
+            weights.append([mine] + [to_group(mine, ahead) for ahead in range(1, parts)])
     else:
         whole = jnp.stack([sub, sub * 0]).astype(jnp.int32)
         got = [lax.psum(steps[0], "grp") if groups > 1 else steps[0]]
-        weights = [renorm_call(whole, got, fast_gate, fast_up, fast_down)]
+        weights.append([renorm_call(whole, got, matrices)])
 
     if halved:
         attended = attention_call(which, query_pieces, pieces, [], None, 1)

time: 215 us -> 226 us (1.051)
  the two profiles are of different devices: /device:TPU:25 before, /device:TPU:0 now
where the time goes in v3:
time: 226 us; the launch traced here: 225 us
  starting transfers between devices  72.7 us (32%)
  waiting for transfers between devices  69.2 us (31%)
  Pallas kernels  64.9 us (29%)
  local copies, waits for them, and re-layouts  11.7 us (5%)
  other arithmetic  5.66 us (3%)
    ppermute x12, waiting for transfers between devices, to_group(): lax.ppermute(value, 'grp', [(source, (source + ahead) % groups) for sourc...  32 us
    ppermute x4, starting transfers between devices, planned(): early.append(lax.ppermute(late, 'grp', links))  28.5 us
    pallas_call x2, Pallas kernels, attention_call(): pl.pallas_call(functools.partial(attention_body, run=run, early=len(early...  25.8 us
    ppermute x14, waiting for transfers between devices, sent(): return lax.ppermute(piece, ('sub', 'head'), links)  24.4 us
    ppermute x12, starting transfers between devices, to_group(): lax.ppermute(value, 'grp', [(source, (source + ahead) % groups) for sourc...  23.4 us
    ppermute x14, starting transfers between devices, sent(): return lax.ppermute(piece, ('sub', 'head'), links)  16.6 us
    ppermute x6, waiting for transfers between devices, to_sub(): lax.ppermute(value, 'sub', [(source, source ^ over) for source in range(s...  12.8 us
    pallas_call x2, Pallas kernels, update_call(): pl.pallas_call(functools.partial(update_body, overs=overs, before=bool(pa...  12.7 us
  transfers between devices with their start and end apart: 36, of which 8 were waited for; matrix products, arithmetic and copies ran while one was open for 3% of the time, Pallas kernels for 27%

profile of v3, /device:TPU:0, one launch (start us, length us, event | category | flops | bytes accessed | tf_op | source)
XLA Modules:
  0.0 224.9 jit_solution(4585395267143262131)
XLA Ops:
  0.1 1.8 spread.7
  1.9 3.1 %collective-permute-start.7 = (bf16[2,256,512]{2,1,0:T(8,128)(2,1)S(1)}, bf16[2,256,512]{2,1,0:T(8,128)(2,1)S(1)}, u32[]{:S(2)}, u32[]{:S(2)}) collective-permute-start(bf16[2,256,512]{2,1,0:T(8,128)(2,1)S(1)} %get-tuple-element.40), channel_id=1, source_target_pairs={{0,1},{1,0},{2,3},{3,2},{4,5},{5,4},{6,7},{7,6},{8,9},{9,8},{10,11... | collective-permute-start | bytes 1572872 | tf_op jit(solution)/shard_map/ppermute | solution.py:402
  4.9 1.5 collective-permute-start.10
  8.4 2.6 %spread.6 = (bf16[2,256,512]{2,1,0:T(8,128)(2,1)S(1)}, bf16[2,256,512]{2,1,0:T(8,128)(2,1)}) custom-call(s32[3]{0:T(128)S(1)} %pad_add_fusion.which, bf16[256,4096]{1,0:T(8,128)(2,1)} %rest_0_.11, bf16[256,4096]{1,0:T(8,128)(2,1)} %rest_1_.8), custom_call_target="tpu_custom_call" | custom-call | flops 524288 | bytes 2097152 | tf_op jit(solution)/shard_map/spread/pallas_call | solution.py:344
  10.9 2.8 %spread.8 = (bf16[2,256,512]{2,1,0:T(8,128)(2,1)}, bf16[2,256,512]{2,1,0:T(8,128)(2,1)}) custom-call(s32[3]{0:T(128)S(1)} %pad_add_fusion.which, bf16[256,4096]{1,0:T(8,128)(2,1)} %rest_0_.11, bf16[256,4096]{1,0:T(8,128)(2,1)} %rest_1_.8), custom_call_target="tpu_custom_call" | custom-call | flops 524288 | bytes 2097152 | tf_op jit(solution)/shard_map/spread/pallas_call | solution.py:344
  13.8 1.8 spread.9
  17.1 2.1 spread.5
  26.2 1.3 copy.13.rate_ref
  27.5 1.5 collective-permute-start.9
  30.1 1.6 collective-permute-start
  31.6 8.8 %collective-permute-done.11.rest_13_.rest_4_ = bf16[2,256,512]{2,1,0:T(8,128)(2,1)} collective-permute-done((bf16[2,256,512]{2,1,0:T(8,128)(2,1)}, bf16[2,256,512]{2,1,0:T(8,128)(2,1)}, u32[]{:S(2)}, u32[]{:S(2)}) %collective-permute-start.11) | collective-permute-done | bytes 524320 | tf_op jit(solution)/shard_map/ppermute | solution.py:402
  40.4 9.2 %collective-permute-done.12.rest_14_.rest_5_ = bf16[2,256,512]{2,1,0:T(8,128)(2,1)} collective-permute-done((bf16[2,256,512]{2,1,0:T(8,128)(2,1)}, bf16[2,256,512]{2,1,0:T(8,128)(2,1)}, u32[]{:S(2)}, u32[]{:S(2)}) %collective-permute-start.12) | collective-permute-done | bytes 524320 | tf_op jit(solution)/shard_map/ppermute | solution.py:402
  49.6 2.2 collective-permute-start.2
  53.1 9.0 %update.2 = (f32[3,512,512]{2,1,0:T(8,128)S(1)}, bf16[3,512,512]{2,1,0:T(8,128)(2,1)S(1)}) custom-call(s32[3]{0:T(128)S(1)} %pad_add_fusion.which, f32[2048,1]{1,0:T(8,128)S(1)} %copy-done.6, bf16[2,256,512]{2,1,0:T(8,128)(2,1)S(1)} %get-tuple-element.39.rest_8_.rest_0_, bf16[2,256,512]{2,1,0:T(8,128)(2,1)S(1)} %collective-permute-done.7.rest_9_.rest_1_, ...), custom_call_target="tpu_custom_call" | custom-call | flops 4831838208 | bytes 7864320 | tf_op jit(solution)/shard_map/update/pallas_call | solution.py:214
  64.2 3.7 %update.3 = (f32[2,512,128]{2,1,0:T(8,128)S(1)}, bf16[2,512,128]{2,1,0:T(8,128)(2,1)S(1)}, bf16[2,512,128]{2,1,0:T(8,128)(2,1)S(1)}, bf16[2,512,128]{2,1,0:T(8,1...) custom-call(s32[3]{0:T(128)S(1)} %pad_add_fusion.which, ...), custom_call_target="tpu_custom_call" | custom-call | flops 1610612736 | bytes 5767168 | tf_op jit(solution)/shard_map/update/pallas_call | solution.py:214
  68.0 1.9 broadcast_select_fusion.2
  70.0 2.7 %collective-permute-start.6 = (bf16[1,256,512]{2,1,0:T(8,128)(2,1)S(1)}, bf16[1,256,512]{2,1,0:T(8,128)(2,1)S(1)}, u32[]{:S(2)}, u32[]{:S(2)}) collective-permute-start(bf16[1,256,512]{2,1,0:T(8,128)(2,1)S(1)} %get-tuple-element.38), channel_id=1, source_target_pairs={{0,7},{1,6},{2,5},{3,4},{4,3},{5,2},{6,1},{7,0},{8,15},{9,14},{10,... | collective-permute-start | bytes 786440 | tf_op jit(solution)/shard_map/ppermute | solution.py:402
  72.7 6.3 %collective-permute-done.2.rest_3_.rest_1_ = bf16[1,256,512]{2,1,0:T(8,128)(2,1)S(1)} collective-permute-done((bf16[1,256,512]{2,1,0:T(8,128)(2,1)}, bf16[1,256,512]{2,1,0:T(8,128)(2,1)S(1)}, u32[]{:S(2)}, u32[]{:S(2)}) %collective-permute-start.2) | collective-permute-done | bytes 262176 | tf_op jit(solution)/shard_map/ppermute | solution.py:402
  79.0 1.6 collective-permute-start.27
  80.6 2.6 %collective-permute-start.28 = (bf16[1,512,128]{2,1,0:T(8,128)(2,1)S(1)}, bf16[1,512,128]{2,1,0:T(8,128)(2,1)S(1)}, u32[]{:S(2)}, u32[]{:S(2)}) collective-permute-start(bf16[1,512,128]{2,1,0:T(8,128)(2,1)S(1)} %get-tuple-element.55), channel_id=1, source_target_pairs={{0,16},{8,24},{16,0},{24,8},{1,17},{9,25},{17,1},{25,9},{2,18},{10... | collective-permute-start | bytes 393224 | tf_op jit(solution)/shard_map/ppermute | solution.py:431
  83.2 1.3 collective-permute-start.29
  84.5 1.9 broadcast_select_fusion.1
  86.5 2.6 %collective-permute-start.14 = (bf16[2,256,512]{2,1,0:T(8,128)(2,1)}, bf16[2,256,512]{2,1,0:T(8,128)(2,1)S(1)}, u32[]{:S(2)}, u32[]{:S(2)}) collective-permute-start(bf16[2,256,512]{2,1,0:T(8,128)(2,1)} %broadcast_select_fusion.3), channel_id=1, source_target_pairs={{0,8},{8,16},{16,24},{1,9},{9,17},{17,25},{2,10},{10,18},{18,26},{... | collective-permute-start | bytes 1572872 | tf_op jit(solution)/shard_map/ppermute | solution.py:455
  89.1 2.1 collective-permute-start.15
  92.2 1.5 collective-permute-start.22
  93.7 3.7 %collective-permute-start.23 = (bf16[2,512,128]{2,1,0:T(8,128)(2,1)S(1)}, bf16[2,512,128]{2,1,0:T(8,128)(2,1)S(1)}, u32[]{:S(2)}, u32[]{:S(2)}) collective-permute-start(bf16[2,512,128]{2,1,0:T(8,128)(2,1)S(1)} %get-tuple-element.52), channel_id=1, source_target_pairs={{0,24},{8,0},{16,8},{24,16},{1,25},{9,1},{17,9},{25,17},{2,26},{10... | collective-permute-start | bytes 786440 | tf_op jit(solution)/shard_map/ppermute | solution.py:431
  98.2 20.2 %collective-permute-done.21.rest_3_ = bf16[2,512,128]{2,1,0:T(8,128)(2,1)S(1)} collective-permute-done((bf16[2,512,128]{2,1,0:T(8,128)(2,1)S(1)}, bf16[2,512,128]{2,1,0:T(8,128)(2,1)S(1)}, u32[]{:S(2)}, u32[]{:S(2)}) %collective-permute-start.21) | collective-permute-done | bytes 262176 | tf_op jit(solution)/shard_map/ppermute | solution.py:431
  118.4 17.4 %collective-permute-start.16 = (bf16[2,256,512]{2,1,0:T(8,128)(2,1)}, bf16[2,256,512]{2,1,0:T(8,128)(2,1)S(1)}, u32[]{:S(2)}, u32[]{:S(2)}) collective-permute-start(bf16[2,256,512]{2,1,0:T(8,128)(2,1)} %broadcast_select_fusion.1), channel_id=1, source_target_pairs={{0,8},{8,16},{16,24},{1,9},{9,17},{17,25},{2,10},{10,18},{18,26},{... | collective-permute-start | bytes 1572872 | tf_op jit(solution)/shard_map/ppermute | solution.py:455
  135.8 6.4 %collective-permute-start.17 = (bf16[2,256,512]{2,1,0:T(8,128)(2,1)}, bf16[2,256,512]{2,1,0:T(8,128)(2,1)}, u32[]{:S(2)}, u32[]{:S(2)}) collective-permute-start(bf16[2,256,512]{2,1,0:T(8,128)(2,1)} %broadcast_select_fusion), channel_id=1, source_target_pairs={{0,8},{8,16},{16,24},{1,9},{9,17},{17,25},{2,10},{10,18},{18,26},{... | collective-permute-start | bytes 1572872 | tf_op jit(solution)/shard_map/ppermute | solution.py:455
  142.2 1.7 renorm.3.rest_6_
  146.4 1.9 renorm.2.rest_2_
  148.3 11.6 %collective-permute-done.30.rest_7_ = bf16[1,512,128]{2,1,0:T(8,128)(2,1)S(1)} collective-permute-done((bf16[1,512,128]{2,1,0:T(8,128)(2,1)S(1)}, bf16[1,512,128]{2,1,0:T(8,128)(2,1)S(1)}, u32[]{:S(2)}, u32[]{:S(2)}) %collective-permute-start.30) | collective-permute-done | bytes 131104 | tf_op jit(solution)/shard_map/ppermute | solution.py:431
  159.8 4.1 %collective-permute-start.24 = (bf16[2,512,128]{2,1,0:T(8,128)(2,1)S(1)}, bf16[2,512,128]{2,1,0:T(8,128)(2,1)S(1)}, u32[]{:S(2)}, u32[]{:S(2)}) collective-permute-start(bf16[2,512,128]{2,1,0:T(8,128)(2,1)S(1)} %renorm.2.rest_2_), channel_id=1, source_target_pairs={{0,8},{8,16},{16,24},{24,0},{1,9},{9,17},{17,25},{25,1},{2,10},{10... | collective-permute-start | bytes 786440 | tf_op jit(solution)/shard_map/ppermute | solution.py:431
  164.0 3.3 %collective-permute-start.25 = (bf16[2,512,128]{2,1,0:T(8,128)(2,1)S(1)}, bf16[2,512,128]{2,1,0:T(8,128)(2,1)S(1)}, u32[]{:S(2)}, u32[]{:S(2)}) collective-permute-start(bf16[2,512,128]{2,1,0:T(8,128)(2,1)S(1)} %renorm.2.rest_2_), channel_id=1, source_target_pairs={{0,16},{8,24},{16,0},{24,8},{1,17},{9,25},{17,1},{25,9},{2,18},{10... | collective-permute-start | bytes 786440 | tf_op jit(solution)/shard_map/ppermute | solution.py:431
  167.3 1.5 collective-permute-start.26
  168.8 12.7 %attention.2.rest_20_ = f32[2048,512]{1,0:T(8,128)S(1)} custom-call(s32[3]{0:T(128)S(1)} %pad_add_fusion.which, bf16[1,256,512]{2,1,0:T(8,128)(2,1)} %copy-done.8, bf16[1,256,512]{2,1,0:T(8,128)(2,1)} %copy-done.10, bf16[1,256,512]{2,1,0:T(8,128)(2,1)} %copy-done.12, bf16[1,256,512]{2,1,0:T(8,128)(2,1)} %copy-done.14, bf16[1,256,512]{2,1,0:T(8,128)(2,1)} %copy-done.16, ...), custom_call_target="tpu_custom_call" | custom-call | flops 2684354560 | bytes 14680064 | tf_op jit(solution)/shard_map/attention/pallas_call | solution.py:116
  181.7 2.9 %collective-permute-start.32 = (bf16[1,512,128]{2,1,0:T(8,128)(2,1)S(1)}, bf16[1,512,128]{2,1,0:T(8,128)(2,1)S(1)}, u32[]{:S(2)}, u32[]{:S(2)}) collective-permute-start(bf16[1,512,128]{2,1,0:T(8,128)(2,1)S(1)} %renorm.3.rest_6_), channel_id=1, source_target_pairs={{0,24},{8,0},{16,8},{24,16},{1,25},{9,1},{17,9},{25,17},{2,26},{10... | collective-permute-start | bytes 393224 | tf_op jit(solution)/shard_map/ppermute | solution.py:431
  184.6 13.1 %attention.3.attended_ref = f32[2048,512]{1,0:T(8,128)S(1)} custom-call(s32[3]{0:T(128)S(1)} %pad_add_fusion.which, bf16[1,256,512]{2,1,0:T(8,128)(2,1)} %copy-done.8, bf16[1,256,512]{2,1,0:T(8,128)(2,1)} %copy-done.10, bf16[1,256,512]{2,1,0:T(8,128)(2,1)} %copy-done.12, bf16[1,256,512]{2,1,0:T(8,128)(2,1)} %copy-done.14, ...), custom_call_target="tpu_custom_call", output_to_operand_aliasing={{}: (21, {})} | custom-call | flops 2684354560 | bytes 14680064 | tf_op jit(solution)/shard_map/attention/pallas_call | solution.py:116
  197.8 1.9 readout.5
  199.8 1.9 readout.7
  202.4 1.9 readout.4
  204.2 1.6 collective-permute-start.33
  205.8 1.9 readout.6.rest_0_
  207.7 1.5 join.3.rest_1_
  209.2 4.7 %collective-permute-done.34.rest_0_ = bf16[512,512]{1,0:T(8,128)(2,1)S(1)} collective-permute-done((bf16[512,512]{1,0:T(8,128)(2,1)S(1)}, bf16[512,512]{1,0:T(8,128)(2,1)S(1)}, u32[]{:S(2)}, u32[]{:S(2)}) %collective-permute-start.34) | collective-permute-done | bytes 524320 | tf_op jit(solution)/shard_map/ppermute | solution.py:428
  214.0 1.3 join.4.rest_1_
  215.3 8.0 %collective-permute-done.33.rest_0_ = bf16[512,512]{1,0:T(8,128)(2,1)S(1)} collective-permute-done((bf16[512,512]{1,0:T(8,128)(2,1)S(1)}, bf16[512,512]{1,0:T(8,128)(2,1)S(1)}, u32[]{:S(2)}, u32[]{:S(2)}) %collective-permute-start.33) | collective-permute-done | bytes 524320 | tf_op jit(solution)/shard_map/ppermute | solution.py:428
  223.4 1.3 join.5
  (135 shorter events, 20.0 us)
Async XLA Ops:
  1.9 25.6 %collective-permute-start.7 = (bf16[2,256,512]{2,1,0:T(8,128)(2,1)S(1)}, bf16[2,256,512]{2,1,0:T(8,128)(2,1)S(1)}, u32[]{:S(2)}, u32[]{:S(2)}) collective-permute-start(bf16[2,256,512]{2,1,0:T(8,128)(2,1)S(1)} %get-tuple-element.40), channel_id=1, source_target_pairs={{0,1},{1,0},{2,3},{3,2},{4,5},{5,4},{6,7},{7,6},{8,9},{9,8},{10,11... | collective-permute-start | bytes 1572872 | tf_op jit(solution)/shard_map/ppermute | solution.py:402
  4.9 24.1 %collective-permute-start.10 = (bf16[2,256,512]{2,1,0:T(8,128)(2,1)S(1)}, bf16[2,256,512]{2,1,0:T(8,128)(2,1)S(1)}, u32[]{:S(2)}, u32[]{:S(2)}) collective-permute-start(bf16[2,256,512]{2,1,0:T(8,128)(2,1)S(1)} %get-tuple-element.43), channel_id=1, source_target_pairs={{0,4},{1,5},{2,6},{3,7},{4,0},{5,1},{6,2},{7,3},{8,12},{9,13},{10,... | collective-permute-start | bytes 1572872 | tf_op jit(solution)/shard_map/ppermute | solution.py:402
  6.4 17.9 %collective-permute-start.20 = (f32[512]{0:T(512)S(1)}, f32[512]{0:T(512)S(1)}, u32[]{:S(2)}, u32[]{:S(2)}) collective-permute-start(f32[512]{0:T(512)S(1)} %bitcast.31), channel_id=1, source_target_pairs={{0,6},{2,4},{4,2},{6,0},{1,7},{3,5},{5,3},{7,1},{8,14},{10,12},{12... | collective-permute-start | bytes 6152 | tf_op jit(solution)/shard_map/ppermute | solution.py:428
  6.5 17.8 %collective-permute-start.19 = (f32[512]{0:T(512)S(1)}, f32[512]{0:T(512)S(1)}, u32[]{:S(2)}, u32[]{:S(2)}) collective-permute-start(f32[512]{0:T(512)S(1)} %bitcast.30), channel_id=1, source_target_pairs={{0,4},{2,6},{4,0},{6,2},{1,5},{3,7},{5,1},{7,3},{8,12},{10,14},{12... | collective-permute-start | bytes 6152 | tf_op jit(solution)/shard_map/ppermute | solution.py:428
  7.4 17.6 %collective-permute-start.18 = (f32[512]{0:T(512)S(1)}, f32[512]{0:T(512)S(1)}, u32[]{:S(2)}, u32[]{:S(2)}) collective-permute-start(f32[512]{0:T(512)S(1)} %bitcast.29), channel_id=1, source_target_pairs={{0,2},{2,0},{4,6},{6,4},{1,3},{3,1},{5,7},{7,5},{8,10},{10,8},{12,... | collective-permute-start | bytes 6152 | tf_op jit(solution)/shard_map/ppermute | solution.py:428
  10.9 40.9 %copy-start.4 = (bf16[2,256,512]{2,1,0:T(8,128)(2,1)}, bf16[2,256,512]{2,1,0:T(8,128)(2,1)S(1)}, u32[]{:S(2)}) copy-start(bf16[2,256,512]{2,1,0:T(8,128)(2,1)S(1)} %get-tuple-element.39.rest_8_.rest_0_) | copy-start | bytes 1572868
  24.3 5.8 %collective-permute-start.8 = (bf16[2,256,512]{2,1,0:T(8,128)(2,1)}, bf16[2,256,512]{2,1,0:T(8,128)(2,1)S(1)}, u32[]{:S(2)}, u32[]{:S(2)}) collective-permute-start(bf16[2,256,512]{2,1,0:T(8,128)(2,1)} %get-tuple-element.41), channel_id=1, source_target_pairs={{0,2},{1,3},{2,0},{3,1},{4,6},{5,7},{6,4},{7,5},{8,10},{9,11},{10,... | collective-permute-start | bytes 1572872 | tf_op jit(solution)/shard_map/ppermute | solution.py:402
  24.3 16.1 %collective-permute-start.11 = (bf16[2,256,512]{2,1,0:T(8,128)(2,1)}, bf16[2,256,512]{2,1,0:T(8,128)(2,1)}, u32[]{:S(2)}, u32[]{:S(2)}) collective-permute-start(bf16[2,256,512]{2,1,0:T(8,128)(2,1)} %get-tuple-element.44), channel_id=1, source_target_pairs={{0,5},{1,4},{2,7},{3,6},{4,1},{5,0},{6,3},{7,2},{8,13},{9,12},{10,... | collective-permute-start | bytes 1572872 | tf_op jit(solution)/shard_map/ppermute | solution.py:402
  25.0 24.6 %collective-permute-start.12 = (bf16[2,256,512]{2,1,0:T(8,128)(2,1)}, bf16[2,256,512]{2,1,0:T(8,128)(2,1)}, u32[]{:S(2)}, u32[]{:S(2)}) collective-permute-start(bf16[2,256,512]{2,1,0:T(8,128)(2,1)} %get-tuple-element.45), channel_id=1, source_target_pairs={{0,6},{1,7},{2,4},{3,5},{4,2},{5,3},{6,0},{7,1},{8,14},{9,15},{10,... | collective-permute-start | bytes 1572872 | tf_op jit(solution)/shard_map/ppermute | solution.py:402
  27.5 40.4 %copy-start.2 = (bf16[2,256,512]{2,1,0:T(8,128)(2,1)}, bf16[2,256,512]{2,1,0:T(8,128)(2,1)S(1)}, u32[]{:S(2)}) copy-start(bf16[2,256,512]{2,1,0:T(8,128)(2,1)S(1)} %collective-permute-done.7.rest_9_.rest_1_) | copy-start | bytes 1572868
  27.5 34.6 %collective-permute-start.9 = (bf16[2,256,512]{2,1,0:T(8,128)(2,1)}, bf16[2,256,512]{2,1,0:T(8,128)(2,1)S(1)}, u32[]{:S(2)}, u32[]{:S(2)}) collective-permute-start(bf16[2,256,512]{2,1,0:T(8,128)(2,1)} %copy-done.27), channel_id=1, source_target_pairs={{0,3},{1,2},{2,1},{3,0},{4,7},{5,6},{6,5},{7,4},{8,11},{9,10},{10,... | collective-permute-start | bytes 1572872 | tf_op jit(solution)/shard_map/ppermute | solution.py:402
  29.0 33.9 %collective-permute-start.13 = (bf16[2,256,512]{2,1,0:T(8,128)(2,1)}, bf16[2,256,512]{2,1,0:T(8,128)(2,1)S(1)}, u32[]{:S(2)}, u32[]{:S(2)}) collective-permute-start(bf16[2,256,512]{2,1,0:T(8,128)(2,1)} %copy-done.26), channel_id=1, source_target_pairs={{0,7},{1,6},{2,5},{3,4},{4,3},{5,2},{6,1},{7,0},{8,15},{9,14},{10,... | collective-permute-start | bytes 1572872 | tf_op jit(solution)/shard_map/ppermute | solution.py:402
  30.1 54.5 %copy-start.5 = (bf16[2,256,512]{2,1,0:T(8,128)(2,1)}, bf16[2,256,512]{2,1,0:T(8,128)(2,1)S(1)}, u32[]{:S(2)}) copy-start(bf16[2,256,512]{2,1,0:T(8,128)(2,1)S(1)} %collective-permute-done.8.rest_10_.rest_2_) | copy-start | bytes 1572868
  30.1 39.8 %collective-permute-start = (bf16[1,256,512]{2,1,0:T(8,128)(2,1)}, bf16[1,256,512]{2,1,0:T(8,128)(2,1)S(1)}, u32[]{:S(2)}, u32[]{:S(2)}) collective-permute-start(bf16[1,256,512]{2,1,0:T(8,128)(2,1)} %copy-done.36), channel_id=1, source_target_pairs={{0,1},{1,0},{2,3},{3,2},{4,5},{5,4},{6,7},{7,6},{8,9},{9,8},{10,11... | collective-permute-start | bytes 786440 | tf_op jit(solution)/shard_map/ppermute | solution.py:402
  40.4 29.6 %collective-permute-start.1 = (bf16[1,256,512]{2,1,0:T(8,128)(2,1)}, bf16[1,256,512]{2,1,0:T(8,128)(2,1)S(1)}, u32[]{:S(2)}, u32[]{:S(2)}) collective-permute-start(bf16[1,256,512]{2,1,0:T(8,128)(2,1)} %copy-done.35), channel_id=1, source_target_pairs={{0,2},{1,3},{2,0},{3,1},{4,6},{5,7},{6,4},{7,5},{8,10},{9,11},{10,... | collective-permute-start | bytes 786440 | tf_op jit(solution)/shard_map/ppermute | solution.py:402
  49.6 29.4 %collective-permute-start.2 = (bf16[1,256,512]{2,1,0:T(8,128)(2,1)}, bf16[1,256,512]{2,1,0:T(8,128)(2,1)S(1)}, u32[]{:S(2)}, u32[]{:S(2)}) collective-permute-start(bf16[1,256,512]{2,1,0:T(8,128)(2,1)} %copy-done.34), channel_id=1, source_target_pairs={{0,3},{1,2},{2,1},{3,0},{4,7},{5,6},{6,5},{7,4},{8,11},{9,10},{10,... | collective-permute-start | bytes 786440 | tf_op jit(solution)/shard_map/ppermute | solution.py:402
  62.1 35.2 %copy-start = (bf16[2,256,512]{2,1,0:T(8,128)(2,1)}, bf16[2,256,512]{2,1,0:T(8,128)(2,1)S(1)}, u32[]{:S(2)}) copy-start(bf16[2,256,512]{2,1,0:T(8,128)(2,1)S(1)} %collective-permute-done.9.rest_11_.rest_0_) | copy-start | bytes 1572868
  62.1 18.5 %collective-permute-start.3 = (bf16[1,256,512]{2,1,0:T(8,128)(2,1)S(1)}, bf16[1,256,512]{2,1,0:T(8,128)(2,1)S(1)}, u32[]{:S(2)}, u32[]{:S(2)}) collective-permute-start(bf16[1,256,512]{2,1,0:T(8,128)(2,1)S(1)} %copy-done.33), channel_id=1, source_target_pairs={{0,4},{1,5},{2,6},{3,7},{4,0},{5,1},{6,2},{7,3},{8,12},{9,13},{10,... | collective-permute-start | bytes 786440 | tf_op jit(solution)/shard_map/ppermute | solution.py:402
  62.9 34.5 %copy-start.1 = (bf16[2,256,512]{2,1,0:T(8,128)(2,1)}, bf16[2,256,512]{2,1,0:T(8,128)(2,1)S(1)}, u32[]{:S(2)}) copy-start(bf16[2,256,512]{2,1,0:T(8,128)(2,1)S(1)} %collective-permute-done.13.rest_15_.rest_1_) | copy-start | bytes 1572868
  62.9 20.3 %collective-permute-start.4 = (bf16[1,256,512]{2,1,0:T(8,128)(2,1)S(1)}, bf16[1,256,512]{2,1,0:T(8,128)(2,1)S(1)}, u32[]{:S(2)}, u32[]{:S(2)}) collective-permute-start(bf16[1,256,512]{2,1,0:T(8,128)(2,1)S(1)} %copy-done.31), channel_id=1, source_target_pairs={{0,5},{1,4},{2,7},{3,6},{4,1},{5,0},{6,3},{7,2},{8,13},{9,12},{10,... | collective-permute-start | bytes 786440 | tf_op jit(solution)/shard_map/ppermute | solution.py:402
  69.9 74.0 %copy-start.10 = (bf16[1,256,512]{2,1,0:T(8,128)(2,1)}, bf16[1,256,512]{2,1,0:T(8,128)(2,1)S(1)}, u32[]{:S(2)}) copy-start(bf16[1,256,512]{2,1,0:T(8,128)(2,1)S(1)} %collective-permute-done.rest_1_) | copy-start | bytes 786436
  69.9 16.6 %collective-permute-start.5 = (bf16[1,256,512]{2,1,0:T(8,128)(2,1)S(1)}, bf16[1,256,512]{2,1,0:T(8,128)(2,1)S(1)}, u32[]{:S(2)}, u32[]{:S(2)}) collective-permute-start(bf16[1,256,512]{2,1,0:T(8,128)(2,1)S(1)} %copy-done.29), channel_id=1, source_target_pairs={{0,6},{1,7},{2,4},{3,5},{4,2},{5,3},{6,0},{7,1},{8,14},{9,15},{10,... | collective-permute-start | bytes 786440 | tf_op jit(solution)/shard_map/ppermute | solution.py:402
  70.0 73.9 %copy-start.12 = (bf16[1,256,512]{2,1,0:T(8,128)(2,1)}, bf16[1,256,512]{2,1,0:T(8,128)(2,1)S(1)}, u32[]{:S(2)}) copy-start(bf16[1,256,512]{2,1,0:T(8,128)(2,1)S(1)} %collective-permute-done.1.rest_2_.rest_0_) | copy-start | bytes 786436
  70.0 19.1 %collective-permute-start.6 = (bf16[1,256,512]{2,1,0:T(8,128)(2,1)S(1)}, bf16[1,256,512]{2,1,0:T(8,128)(2,1)S(1)}, u32[]{:S(2)}, u32[]{:S(2)}) collective-permute-start(bf16[1,256,512]{2,1,0:T(8,128)(2,1)S(1)} %get-tuple-element.38), channel_id=1, source_target_pairs={{0,7},{1,6},{2,5},{3,4},{4,3},{5,2},{6,1},{7,0},{8,15},{9,14},{10,... | collective-permute-start | bytes 786440 | tf_op jit(solution)/shard_map/ppermute | solution.py:402
  79.0 64.9 %copy-start.14 = (bf16[1,256,512]{2,1,0:T(8,128)(2,1)}, bf16[1,256,512]{2,1,0:T(8,128)(2,1)S(1)}, u32[]{:S(2)}) copy-start(bf16[1,256,512]{2,1,0:T(8,128)(2,1)S(1)} %collective-permute-done.2.rest_3_.rest_1_) | copy-start | bytes 786436
  79.0 12.2 %collective-permute-start.27 = (bf16[1,512,128]{2,1,0:T(8,128)(2,1)S(1)}, bf16[1,512,128]{2,1,0:T(8,128)(2,1)S(1)}, u32[]{:S(2)}, u32[]{:S(2)}) collective-permute-start(bf16[1,512,128]{2,1,0:T(8,128)(2,1)S(1)} %get-tuple-element.54), channel_id=1, source_target_pairs={{0,8},{8,16},{16,24},{24,0},{1,9},{9,17},{17,25},{25,1},{2,10},{10... | collective-permute-start | bytes 393224 | tf_op jit(solution)/shard_map/ppermute | solution.py:431
  80.6 63.3 %copy-start.16 = (bf16[1,256,512]{2,1,0:T(8,128)(2,1)}, bf16[1,256,512]{2,1,0:T(8,128)(2,1)S(1)}, u32[]{:S(2)}) copy-start(bf16[1,256,512]{2,1,0:T(8,128)(2,1)S(1)} %collective-permute-done.3.rest_4_.rest_0_) | copy-start | bytes 786436
  80.6 11.6 %collective-permute-start.28 = (bf16[1,512,128]{2,1,0:T(8,128)(2,1)S(1)}, bf16[1,512,128]{2,1,0:T(8,128)(2,1)S(1)}, u32[]{:S(2)}, u32[]{:S(2)}) collective-permute-start(bf16[1,512,128]{2,1,0:T(8,128)(2,1)S(1)} %get-tuple-element.55), channel_id=1, source_target_pairs={{0,16},{8,24},{16,0},{24,8},{1,17},{9,25},{17,1},{25,9},{2,18},{10... | collective-permute-start | bytes 393224 | tf_op jit(solution)/shard_map/ppermute | solution.py:431
  83.2 60.7 %copy-start.18 = (bf16[1,256,512]{2,1,0:T(8,128)(2,1)}, bf16[1,256,512]{2,1,0:T(8,128)(2,1)S(1)}, u32[]{:S(2)}) copy-start(bf16[1,256,512]{2,1,0:T(8,128)(2,1)S(1)} %collective-permute-done.4.rest_5_.rest_1_) | copy-start | bytes 786436
  83.2 10.5 %collective-permute-start.29 = (bf16[1,512,128]{2,1,0:T(8,128)(2,1)S(1)}, bf16[1,512,128]{2,1,0:T(8,128)(2,1)S(1)}, u32[]{:S(2)}, u32[]{:S(2)}) collective-permute-start(bf16[1,512,128]{2,1,0:T(8,128)(2,1)S(1)} %get-tuple-element.56), channel_id=1, source_target_pairs={{0,24},{8,0},{16,8},{24,16},{1,25},{9,1},{17,9},{25,17},{2,26},{10... | collective-permute-start | bytes 393224 | tf_op jit(solution)/shard_map/ppermute | solution.py:431
  86.5 57.5 %copy-start.20 = (bf16[1,256,512]{2,1,0:T(8,128)(2,1)}, bf16[1,256,512]{2,1,0:T(8,128)(2,1)S(1)}, u32[]{:S(2)}) copy-start(bf16[1,256,512]{2,1,0:T(8,128)(2,1)S(1)} %collective-permute-done.5.rest_6_.rest_0_) | copy-start | bytes 786436
  86.5 77.5 %collective-permute-start.14 = (bf16[2,256,512]{2,1,0:T(8,128)(2,1)}, bf16[2,256,512]{2,1,0:T(8,128)(2,1)S(1)}, u32[]{:S(2)}, u32[]{:S(2)}) collective-permute-start(bf16[2,256,512]{2,1,0:T(8,128)(2,1)} %broadcast_select_fusion.3), channel_id=1, source_target_pairs={{0,8},{8,16},{16,24},{1,9},{9,17},{17,25},{2,10},{10,18},{18,26},{... | collective-permute-start | bytes 1572872 | tf_op jit(solution)/shard_map/ppermute | solution.py:455
  89.1 54.9 %copy-start.22 = (bf16[1,256,512]{2,1,0:T(8,128)(2,1)}, bf16[1,256,512]{2,1,0:T(8,128)(2,1)S(1)}, u32[]{:S(2)}) copy-start(bf16[1,256,512]{2,1,0:T(8,128)(2,1)S(1)} %collective-permute-done.6.rest_7_.rest_1_) | copy-start | bytes 786436
  89.1 78.3 %collective-permute-start.15 = (bf16[2,256,512]{2,1,0:T(8,128)(2,1)}, bf16[2,256,512]{2,1,0:T(8,128)(2,1)S(1)}, u32[]{:S(2)}, u32[]{:S(2)}) collective-permute-start(bf16[2,256,512]{2,1,0:T(8,128)(2,1)} %broadcast_select_fusion.2), channel_id=1, source_target_pairs={{0,8},{8,16},{16,24},{1,9},{9,17},{17,25},{2,10},{10,18},{18,26},{... | collective-permute-start | bytes 1572872 | tf_op jit(solution)/shard_map/ppermute | solution.py:455
  91.2 27.2 %collective-permute-start.21 = (bf16[2,512,128]{2,1,0:T(8,128)(2,1)S(1)}, bf16[2,512,128]{2,1,0:T(8,128)(2,1)S(1)}, u32[]{:S(2)}, u32[]{:S(2)}) collective-permute-start(bf16[2,512,128]{2,1,0:T(8,128)(2,1)S(1)} %get-tuple-element.50), channel_id=1, source_target_pairs={{0,8},{8,16},{16,24},{24,0},{1,9},{9,17},{17,25},{25,1},{2,10},{10... | collective-permute-start | bytes 786440 | tf_op jit(solution)/shard_map/ppermute | solution.py:431
  92.2 43.6 %collective-permute-start.22 = (bf16[2,512,128]{2,1,0:T(8,128)(2,1)S(1)}, bf16[2,512,128]{2,1,0:T(8,128)(2,1)S(1)}, u32[]{:S(2)}, u32[]{:S(2)}) collective-permute-start(bf16[2,512,128]{2,1,0:T(8,128)(2,1)S(1)} %get-tuple-element.51), channel_id=1, source_target_pairs={{0,16},{8,24},{16,0},{24,8},{1,17},{9,25},{17,1},{25,9},{2,18},{10... | collective-permute-start | bytes 786440 | tf_op jit(solution)/shard_map/ppermute | solution.py:431
  93.7 50.3 %collective-permute-start.23 = (bf16[2,512,128]{2,1,0:T(8,128)(2,1)S(1)}, bf16[2,512,128]{2,1,0:T(8,128)(2,1)S(1)}, u32[]{:S(2)}, u32[]{:S(2)}) collective-permute-start(bf16[2,512,128]{2,1,0:T(8,128)(2,1)S(1)} %get-tuple-element.52), channel_id=1, source_target_pairs={{0,24},{8,0},{16,8},{24,16},{1,25},{9,1},{17,9},{25,17},{2,26},{10... | collective-permute-start | bytes 786440 | tf_op jit(solution)/shard_map/ppermute | solution.py:431
  118.4 63.2 %collective-permute-start.16 = (bf16[2,256,512]{2,1,0:T(8,128)(2,1)}, bf16[2,256,512]{2,1,0:T(8,128)(2,1)S(1)}, u32[]{:S(2)}, u32[]{:S(2)}) collective-permute-start(bf16[2,256,512]{2,1,0:T(8,128)(2,1)} %broadcast_select_fusion.1), channel_id=1, source_target_pairs={{0,8},{8,16},{16,24},{1,9},{9,17},{17,25},{2,10},{10,18},{18,26},{... | collective-permute-start | bytes 1572872 | tf_op jit(solution)/shard_map/ppermute | solution.py:455
  135.8 45.9 %collective-permute-start.17 = (bf16[2,256,512]{2,1,0:T(8,128)(2,1)}, bf16[2,256,512]{2,1,0:T(8,128)(2,1)}, u32[]{:S(2)}, u32[]{:S(2)}) collective-permute-start(bf16[2,256,512]{2,1,0:T(8,128)(2,1)} %broadcast_select_fusion), channel_id=1, source_target_pairs={{0,8},{8,16},{16,24},{1,9},{9,17},{17,25},{2,10},{10,18},{18,26},{... | collective-permute-start | bytes 1572872 | tf_op jit(solution)/shard_map/ppermute | solution.py:455
  144.7 15.2 %collective-permute-start.30 = (bf16[1,512,128]{2,1,0:T(8,128)(2,1)S(1)}, bf16[1,512,128]{2,1,0:T(8,128)(2,1)S(1)}, u32[]{:S(2)}, u32[]{:S(2)}) collective-permute-start(bf16[1,512,128]{2,1,0:T(8,128)(2,1)S(1)} %renorm.3.rest_6_), channel_id=1, source_target_pairs={{0,8},{8,16},{16,24},{24,0},{1,9},{9,17},{17,25},{25,1},{2,10},{10... | collective-permute-start | bytes 393224 | tf_op jit(solution)/shard_map/ppermute | solution.py:431
  159.8 37.9 %collective-permute-start.24 = (bf16[2,512,128]{2,1,0:T(8,128)(2,1)S(1)}, bf16[2,512,128]{2,1,0:T(8,128)(2,1)S(1)}, u32[]{:S(2)}, u32[]{:S(2)}) collective-permute-start(bf16[2,512,128]{2,1,0:T(8,128)(2,1)S(1)} %renorm.2.rest_2_), channel_id=1, source_target_pairs={{0,8},{8,16},{16,24},{24,0},{1,9},{9,17},{17,25},{25,1},{2,10},{10... | collective-permute-start | bytes 786440 | tf_op jit(solution)/shard_map/ppermute | solution.py:431
  164.0 33.7 %collective-permute-start.25 = (bf16[2,512,128]{2,1,0:T(8,128)(2,1)S(1)}, bf16[2,512,128]{2,1,0:T(8,128)(2,1)S(1)}, u32[]{:S(2)}, u32[]{:S(2)}) collective-permute-start(bf16[2,512,128]{2,1,0:T(8,128)(2,1)S(1)} %renorm.2.rest_2_), channel_id=1, source_target_pairs={{0,16},{8,24},{16,0},{24,8},{1,17},{9,25},{17,1},{25,9},{2,18},{10... | collective-permute-start | bytes 786440 | tf_op jit(solution)/shard_map/ppermute | solution.py:431
  167.3 30.4 %collective-permute-start.26 = (bf16[2,512,128]{2,1,0:T(8,128)(2,1)S(1)}, bf16[2,512,128]{2,1,0:T(8,128)(2,1)S(1)}, u32[]{:S(2)}, u32[]{:S(2)}) collective-permute-start(bf16[2,512,128]{2,1,0:T(8,128)(2,1)S(1)} %renorm.2.rest_2_), channel_id=1, source_target_pairs={{0,24},{8,0},{16,8},{24,16},{1,25},{9,1},{17,9},{25,17},{2,26},{10... | collective-permute-start | bytes 786440 | tf_op jit(solution)/shard_map/ppermute | solution.py:431
  181.6 16.1 %collective-permute-start.31 = (bf16[1,512,128]{2,1,0:T(8,128)(2,1)S(1)}, bf16[1,512,128]{2,1,0:T(8,128)(2,1)S(1)}, u32[]{:S(2)}, u32[]{:S(2)}) collective-permute-start(bf16[1,512,128]{2,1,0:T(8,128)(2,1)S(1)} %renorm.3.rest_6_), channel_id=1, source_target_pairs={{0,16},{8,24},{16,0},{24,8},{1,17},{9,25},{17,1},{25,9},{2,18},{10... | collective-permute-start | bytes 393224 | tf_op jit(solution)/shard_map/ppermute | solution.py:431
  181.7 16.0 %collective-permute-start.32 = (bf16[1,512,128]{2,1,0:T(8,128)(2,1)S(1)}, bf16[1,512,128]{2,1,0:T(8,128)(2,1)S(1)}, u32[]{:S(2)}, u32[]{:S(2)}) collective-permute-start(bf16[1,512,128]{2,1,0:T(8,128)(2,1)S(1)} %renorm.3.rest_6_), channel_id=1, source_target_pairs={{0,24},{8,0},{16,8},{24,16},{1,25},{9,1},{17,9},{25,17},{2,26},{10... | collective-permute-start | bytes 393224 | tf_op jit(solution)/shard_map/ppermute | solution.py:431
  199.7 14.3 %collective-permute-start.34 = (bf16[512,512]{1,0:T(8,128)(2,1)S(1)}, bf16[512,512]{1,0:T(8,128)(2,1)S(1)}, u32[]{:S(2)}, u32[]{:S(2)}) collective-permute-start(bf16[512,512]{1,0:T(8,128)(2,1)S(1)} %readout.5), channel_id=1, source_target_pairs={{0,6},{2,4},{4,2},{6,0},{1,7},{3,5},{5,3},{7,1},{8,14},{10,12},{12... | collective-permute-start | bytes 1572872 | tf_op jit(solution)/shard_map/ppermute | solution.py:428
  201.7 6.0 %collective-permute-start.35 = (bf16[512,512]{1,0:T(8,128)(2,1)S(1)}, bf16[512,512]{1,0:T(8,128)(2,1)S(1)}, u32[]{:S(2)}, u32[]{:S(2)}) collective-permute-start(bf16[512,512]{1,0:T(8,128)(2,1)S(1)} %readout.7), channel_id=1, source_target_pairs={{0,2},{2,0},{4,6},{6,4},{1,3},{3,1},{5,7},{7,5},{8,10},{10,8},{12,... | collective-permute-start | bytes 1572872 | tf_op jit(solution)/shard_map/ppermute | solution.py:428
  204.2 19.1 %collective-permute-start.33 = (bf16[512,512]{1,0:T(8,128)(2,1)S(1)}, bf16[512,512]{1,0:T(8,128)(2,1)S(1)}, u32[]{:S(2)}, u32[]{:S(2)}) collective-permute-start(bf16[512,512]{1,0:T(8,128)(2,1)S(1)} %readout.4), channel_id=1, source_target_pairs={{0,4},{2,6},{4,0},{6,2},{1,5},{3,7},{5,1},{7,3},{8,12},{10,14},{12... | collective-permute-start | bytes 1572872 | tf_op jit(solution)/shard_map/ppermute | solution.py:428
  (29 other events, 167.8 us)
